TPU v7x, 256 devices: a 8x8x2 block of a 8x8x16 slice. The times are simulated.
256 devices in a mesh: groups: 2 (over z), ep: 64 (over y, x), tp: 2 (over core).
Axes of the slice: x: 8, y: 8, z: 2, core: 2. Of those that a mesh axis runs over, the one named last changes fastest.
The devices are a block of a 8x8x16 slice.
Arguments:
- hidden: bfloat16 [2048, 3584], P(('groups', 'ep'), 'tp'), parts along dimension 0, may hold values from -6 to 6
- routes: int32 [2048, 8], P(('groups', 'ep')), parts along dimension 0, may hold values from 0 to 63, as said below
- router_weight: bfloat16 [3584, 64], P('tp'), may hold values from -0.1875 to 0.1875
- gate_weight: bfloat16 [64, 3584, 1024], P('ep', None, 'tp'), may hold values from -0.09375 to 0.09375
- up_weight: bfloat16 [64, 3584, 1024], P('ep', None, 'tp'), may hold values from -0.09375 to 0.09375
- down_weight: bfloat16 [64, 1024, 3584], P('ep', 'tp'), may hold values from -0.1875 to 0.1875
- q_latent: bfloat16 [512, 64, 512], P(('groups', 'ep'), 'tp'), parts along dimension 0, may hold values from -48 to 48
- q_rope: bfloat16 [512, 64, 64], P(('groups', 'ep'), 'tp'), parts along dimension 0, may hold values from -48 to 48
- cache_latent: bfloat16 [512, 256, 512], P(('groups', 'ep')), parts along dimension 0, may hold values from -4 to 4
- cache_rope: bfloat16 [512, 64, 256], P(('groups', 'ep')), parts along dimension 0, may hold values from -4 to 4
- lengths: int32 [512], P(('groups', 'ep')), parts along dimension 0, may hold values from 16 to 256, as said below
Outputs:
- moe_out: bfloat16 [2048, 3584], P(('groups', 'ep'), 'tp'), parts along dimension 0
- attn_latent: bfloat16 [512, 64, 512], P(('groups', 'ep'), 'tp'), parts along dimension 0
There are 2 independent parts, one for each index of `groups`. A program takes and returns all parts, laid end to end along the dimension named above; an argument that names none is the same for every part. Nothing has to cross between parts.
Inputs may be any that keep to these rules, and one draw needn't show every extreme that they name: `routes`: each row names 8 different experts; in each aligned block of 16 rows (the rows of one index of ep) no expert is named more than 8 times, and one expert, the same in every block, is named exactly 8 times in each block. `lengths`: one sequence has 256 live positions and one has 16.
All inputs are finite; a program needn't handle non-finite values.
Results may differ from a plain program's by a relative error of at most 0.0085.
Values may be sent and summed in bfloat16 or wider, within the bound.
No kernel may reach another device: no remote copies, remote signals or barrier semaphores. Data moves between devices by JAX's collectives and lax.ppermute only.
A program may use at most 128 MiB of HBM per device.

v0:
```python
import math

import jax
import jax.numpy as jnp
from jax import lax
from jax.experimental import pallas as pl
from jax.experimental.pallas import tpu as pltpu
from jax.sharding import PartitionSpec as P


softmax_scale = 192.0 ** (-0.5)
routed_scale = 2.5
pair = ("ep", "tp")


def side_of(devices):
    side = math.isqrt(devices)
    assert side * side == devices
    return side


def flat_index(first, second, core, side):
    row, column = (second, first) if core == 0 else (first, second)
    return (row * side + column) * 2 + core


def first_groups(side):
    return [
        [flat_index(first, second, core, side) for first in range(side)]
        for core in range(2)
        for second in range(side)
    ]


def shifted(value, shift, side):
    moves = []
    for core in range(2):
        for first in range(side):
            for second in range(side):
                target = (second + shift) % side
                moves.append(
                    (flat_index(first, second, core, side), flat_index(first, target, core, side))
                )
    return lax.ppermute(value, pair, moves)


def swapped(value, axis):
    return lax.ppermute(value, axis, [(0, 1), (1, 0)])


def on_chip(kernel, out_shapes, operands, scratch=(), limit=16):
    return pl.pallas_call(
        kernel,
        out_shape=out_shapes,
        in_specs=[
            pl.BlockSpec(memory_space=pltpu.SMEM if a.ndim == 1 else pltpu.VMEM) for a in operands
        ],
        out_specs=jax.tree.map(lambda _: pl.BlockSpec(memory_space=pltpu.VMEM), out_shapes),
        scratch_shapes=list(scratch),
        compiler_params=pltpu.CompilerParams(vmem_limit_bytes=limit * 1024 * 1024),
    )(*operands)


def message_kernel(place_ref, hidden_ref, own_ref, other_ref, mask_ref, message_ref):
    side, _, width = message_ref.shape
    half = hidden_ref.shape[1]
    lanes = width - half
    expert_count = mask_ref.shape[1]
    core, second = place_ref[1], place_ref[2]
    chosen = jnp.where(mask_ref[...] > 0, jax.nn.sigmoid(own_ref[...] + other_ref[...]), 0.0)
    gates = routed_scale * chosen / jnp.sum(chosen, axis=1, keepdims=True)
    parts = jnp.concatenate([part.astype(jnp.float32) for part in split_in_two(gates)], axis=1)
    shape = (2 * expert_count, lanes)
    source = lax.broadcasted_iota(jnp.int32, shape, 0)
    lane = lax.broadcasted_iota(jnp.int32, shape, 1)
    low = (lane >= side).astype(jnp.int32)
    ahead = lax.rem(lane - low * side + second, side)
    scale = jnp.where(core == 0, side, 1)
    base = ahead * scale + low * expert_count
    for first in range(side):
        wanted = base + first * jnp.where(core == 0, 1, side)
        select = jnp.where((lane < 2 * side) & (wanted == source), 1.0, 0.0)
        picked = jnp.dot(
            parts.astype(jnp.bfloat16), select.astype(jnp.bfloat16), preferred_element_type=jnp.float32
        )
        message_ref[first, :, pl.ds(0, half)] = hidden_ref[...]
        message_ref[first, :, pl.ds(half, lanes)] = picked.astype(jnp.bfloat16)


def fetch_kernel(*refs):
    sources, (slot_ref, high_ref, low_ref, _), refs = refs[:3], refs[3:7], refs[7:]
    targets, taking, sems = refs[:3], refs[3], refs[4:]
    copies = [pltpu.make_async_copy(s, t, m) for s, t, m in zip(sources, targets, sems)]
    for copy in copies:
        copy.start()
    line_tokens, side = slot_ref.shape
    slots = taking.shape[1] // side
    slot_iota = lax.broadcasted_iota(jnp.int32, (line_tokens, slots), 1)
    steps = far_to_near(side)
    for place in range(0, side, 2):
        columns = pl.ds(place * slots, 2 * slots)
        pair_of = steps[place : place + 2]
        for index, part_ref in enumerate((high_ref, low_ref)):
            taken = [
                jnp.where(slot_ref[:, s : s + 1] == slot_iota, part_ref[:, s : s + 1], 0.0)
                for s in pair_of
            ]
            taking[pl.ds(index * line_tokens, line_tokens), columns] = jnp.concatenate(
                taken, axis=1
            ).astype(jnp.bfloat16)
    for copy in copies:
        copy.wait()


def fetched(arrays, slot, high, low, after):
    line_tokens, side = slot.shape
    taking_shape = (2 * line_tokens, side * after.shape[0])
    vmem = pl.BlockSpec(memory_space=pltpu.VMEM)
    return pl.pallas_call(
        fetch_kernel,
        out_shape=tuple(pltpu.VMEM(a.shape, a.dtype) for a in arrays)
        + (jax.ShapeDtypeStruct(taking_shape, jnp.bfloat16),),
        in_specs=[pl.BlockSpec(memory_space=pltpu.HBM)] * 3
        + [vmem] * 3
        + [pl.BlockSpec(memory_space=pl.ANY)],
        out_specs=(vmem,) * 4,
        scratch_shapes=[pltpu.SemaphoreType.DMA] * len(arrays),
        compiler_params=pltpu.CompilerParams(vmem_limit_bytes=42 * 1024 * 1024),
        name="fetch_weights",
    )(*arrays, slot, high, low, after)


def select_kernel(slot_ref, line_ref, *part_refs):
    side, line_tokens = slot_ref.shape
    slots, half = part_refs[0].shape
    tokens = line_ref[:, :, :half].reshape(line_tokens, half)
    slot_iota = lax.broadcasted_iota(jnp.int32, (slots, line_tokens), 0)
    for step in range(side):
        placing = (slot_ref[step : step + 1, :] == slot_iota).astype(jnp.float32).astype(jnp.bfloat16)
        rows = jnp.dot(placing, tokens, preferred_element_type=jnp.float32)
        part_refs[step][...] = rows.astype(jnp.bfloat16)


def far_to_near(side):
    return sorted(range(side), key=lambda step: (-min(step, side - step), step))


def by_step(parts):
    steps = far_to_near(len(parts))
    return [parts[steps.index(step)] for step in range(len(parts))]


def expert_kernel(side, start_ref, gate_ref, up_ref, down_ref, *refs):
    own_refs, other_refs = by_step(refs[:side]), by_step(refs[side : 2 * side])
    active_ref, sent_ref, own, other = refs[2 * side :]
    early = early_parts(side)
    slots, half = own_refs[0].shape
    capacity = slots // side
    width = gate_ref.shape[1]
    for step in range(side):
        rows = pl.ds(step * slots, slots)
        own[rows, :] = own_refs[step][...]
        for block in range(side):
            other[pl.ds(step * slots + block * capacity, capacity), :] = other_refs[block][
                pl.ds(step * capacity, capacity), :
            ]
    mine = pl.multiple_of(start_ref[0], 256)
    theirs = pl.multiple_of(half - mine, 256)

    def product(weight_ref, columns):
        return jnp.dot(
            own[...], weight_ref[pl.ds(mine, half), columns], preferred_element_type=jnp.float32
        ) + jnp.dot(
            other[...], weight_ref[pl.ds(theirs, half), columns], preferred_element_type=jnp.float32
        )

    tile = 256
    for column in range(0, width, tile):
        columns = pl.ds(column, tile)
        gate_part = product(gate_ref, columns)
        up_part = product(up_ref, columns)
        active_ref[:, columns] = (jax.nn.silu(gate_part) * up_part).astype(jnp.bfloat16)
    send_blocks(early, theirs, active_ref, down_ref, sent_ref)


def early_parts(side):
    return far_to_near(side)[: side // 2 - 1]


def late_parts(side):
    return far_to_near(side)[side // 2 - 1 :]


def send_blocks(blocks, theirs, active_ref, down_ref, sent_ref):
    count, slots, half = sent_ref.shape
    width = active_ref.shape[1]
    side = active_ref.shape[0] // slots
    capacity = slots // side
    active = active_ref[...].reshape(side, side, capacity, width)
    rows = jnp.concatenate([active[:, block].reshape(slots, width) for block in blocks], axis=0)
    tile = 256
    for column in range(0, half, tile):
        weight = down_ref[:, pl.ds(pl.multiple_of(theirs + column, 256), tile)]
        sent = jnp.dot(rows, weight, preferred_element_type=jnp.float32).astype(jnp.bfloat16)
        sent_ref[:, :, pl.ds(column, tile)] = sent.reshape(count, slots, tile)


def late_kernel(side, start_ref, active_ref, down_ref, sent_ref):
    theirs = pl.multiple_of(sent_ref.shape[2] - start_ref[0], 256)
    send_blocks(late_parts(side), theirs, active_ref, down_ref, sent_ref)


def finish_kernel(steps, start_ref, active_ref, down_ref, arrived_ref, *part_refs):
    slots, half = part_refs[0].shape
    mine = start_ref[0]
    rows = jnp.concatenate([active_ref[pl.ds(step * slots, slots), :] for step in steps], axis=0)
    tile = 256
    for column in range(0, half, tile):
        columns = pl.ds(column, tile)
        weight = down_ref[:, pl.ds(pl.multiple_of(mine + column, 256), tile)]
        kept = jnp.dot(rows, weight, preferred_element_type=jnp.float32)
        for index in range(len(steps)):
            arrived = arrived_ref[index, :, columns].astype(jnp.float32)
            part_refs[index][:, columns] = (
                kept[index * slots : (index + 1) * slots] + arrived
            ).astype(jnp.bfloat16)


def gather_kernel(place, taking_ref, *refs):
    back_refs, (out_ref, rows) = refs[:-2], refs[-2:]
    slots, half = back_refs[0].shape
    depth = len(back_refs) * slots
    for index, back_ref in enumerate(back_refs):
        rows[pl.ds(index * slots, slots), :] = back_ref[...]
    taking = taking_ref[:, place * slots : place * slots + depth]
    line_tokens = taking.shape[0] // 2
    tile = 256
    for column in range(0, half, tile):
        columns = pl.ds(column, tile)
        both = jnp.dot(taking, rows[:, columns], preferred_element_type=jnp.float32)
        out_ref[:, columns] = both[:line_tokens] + both[line_tokens:]


def combine_kernel(place, taking_ref, sofar_ref, *refs):
    back_refs, (out_ref, rows) = refs[:-2], refs[-2:]
    slots, half = back_refs[0].shape
    depth = len(back_refs) * slots
    for index, back_ref in enumerate(back_refs):
        rows[pl.ds(index * slots, slots), :] = back_ref[...]
    taking = taking_ref[:, place * slots : place * slots + depth]
    line_tokens = taking.shape[0] // 2
    tile = 256
    for column in range(0, half, tile):
        columns = pl.ds(column, tile)
        both = jnp.dot(taking, rows[:, columns], preferred_element_type=jnp.float32)
        total = sofar_ref[:, columns] + both[:line_tokens] + both[line_tokens:]
        out_ref[:, :, columns] = total.astype(jnp.bfloat16).reshape(
            out_ref.shape[0], out_ref.shape[1], tile
        )


def split_in_two(value):
    high = value.astype(jnp.bfloat16)
    return high, (value - high.astype(jnp.float32)).astype(jnp.bfloat16)


def attention(q_latent, q_rope, cache_latent, cache_rope, lengths):
    scores = jnp.einsum("bhl,bjl->bhj", q_latent, cache_latent, preferred_element_type=jnp.float32)
    scores = scores + jnp.einsum(
        "bhr,brj->bhj", q_rope, cache_rope, preferred_element_type=jnp.float32
    )
    scores = scores * softmax_scale
    position = jnp.arange(cache_latent.shape[1], dtype=jnp.int32)
    live = position[None, None, :] < lengths[:, None, None]
    scores = jnp.where(live, scores, -jnp.inf)
    highest = jnp.max(scores, axis=2, keepdims=True)
    expo = jnp.where(live, jnp.exp(scores - highest), 0.0)
    attn_probs = (expo / jnp.sum(expo, axis=2, keepdims=True)).astype(jnp.bfloat16)
    attn_latent = jnp.einsum(
        "bhj,bjl->bhl", attn_probs, cache_latent, preferred_element_type=jnp.float32
    )
    return attn_latent.astype(jnp.bfloat16)


def local(
    hidden,
    routes,
    router_weight,
    gate_weight,
    up_weight,
    down_weight,
    q_latent,
    q_rope,
    cache_latent,
    cache_rope,
    lengths,
):
    token_count, top_count = routes.shape
    expert_count = lax.axis_size("ep")
    side = side_of(expert_count)
    capacity = min(token_count, 4 * token_count * top_count // expert_count)
    line_slots = side * capacity
    line_tokens = side * token_count
    half = hidden.shape[1]
    bf16, f32 = jnp.bfloat16, jnp.float32

    core = lax.axis_index("tp")
    place = lax.axis_index("ep")
    row, column = place // side, place % side
    first = jnp.where(core == 0, column, row)
    second = jnp.where(core == 0, row, column)
    start = jnp.stack([core * half, core, second]).astype(jnp.int32)

    expert_iota = jnp.arange(expert_count, dtype=jnp.int32)
    mask = jnp.sum((routes.T[:, :, None] == expert_iota).astype(f32), axis=0)
    partial_logits = jnp.dot(hidden, router_weight, preferred_element_type=f32)
    other_logits = swapped(partial_logits, "tp")

    lanes = 128 * ((2 * side + 127) // 128)
    message = on_chip(
        message_kernel,
        jax.ShapeDtypeStruct((side, token_count, half + lanes), bf16),
        (start, hidden, partial_logits, other_logits, mask),
    )
    message, start = lax.optimization_barrier((message, start))
    line = lax.all_to_all(
        message, pair, 0, 0, axis_index_groups=first_groups(side), tiled=True
    )
    line_gates = line[:, :, half : half + 2 * side].reshape(line_tokens, 2 * side)
    gate_high, gate_low = line_gates[:, :side].astype(f32), line_gates[:, side:].astype(f32)

    picked = gate_high != 0
    token_iota = jnp.arange(line_tokens, dtype=jnp.int32)
    block_of = token_iota // token_count
    before = (token_iota[:, None] > token_iota[None, :]) & (block_of[:, None] == block_of[None, :])
    rank = jnp.dot(before.astype(bf16), picked.astype(bf16), preferred_element_type=f32)
    offset = ((first - block_of + side) % side) * capacity
    slot = jnp.where(picked, offset[:, None] + rank.astype(jnp.int32), -1)
    part_shape = jax.ShapeDtypeStruct((line_slots, half), bf16)
    rows = on_chip(select_kernel, (part_shape,) * side, (slot.T, line))

    order = [step for step in far_to_near(side) if step]
    own, other = [rows[0]] + [None] * (side - 1), [None] * side
    for step in order:
        own[step] = shifted(rows[step], step, side)
    weights = (gate_weight[0], up_weight[0], down_weight[0])
    *weights, taking = fetched(weights, slot, gate_high, gate_low, rows[0])
    other[0] = swapped(own[0], "tp")
    own[order[0]], *weights = lax.optimization_barrier((own[order[0]], *weights))
    for step in order:
        other[step] = swapped(own[step], "tp")
    gate_w, up_w, down_w = weights

    attn_latent = attention(q_latent, q_rope, cache_latent, cache_rope, lengths)

    all_slots = side * line_slots
    rows_scratch = pltpu.VMEM((all_slots, half), bf16)
    early, late = early_parts(side), late_parts(side)
    steps = far_to_near(side)
    active, sent = on_chip(
        lambda *refs: expert_kernel(side, *refs),
        (
            jax.ShapeDtypeStruct((all_slots, gate_w.shape[1]), bf16),
            jax.ShapeDtypeStruct((len(early), line_slots, half), bf16),
        ),
        (start, gate_w, up_w, down_w, *(own[s] for s in steps), *(other[s] for s in steps)),
        (rows_scratch, rows_scratch),
        16,
    )
    early_arrived = swapped(sent, "tp")
    late_sent = on_chip(
        lambda *refs: late_kernel(side, *refs),
        jax.ShapeDtypeStruct((len(late), line_slots, half), bf16),
        (start, active, down_w),
    )
    late_arrived = swapped(late_sent, "tp")
    summed = {}
    for steps_of, arrived in ((early, early_arrived), (late, late_arrived)):
        parts = on_chip(
            lambda *refs, steps_of=steps_of: finish_kernel(steps_of, *refs),
            (part_shape,) * len(steps_of),
            (start, active, down_w, arrived),
        )
        summed.update(zip(steps_of, parts))

    back = {0: summed[0]}
    for step in order:
        back[step] = shifted(summed[step], -step, side)
    cut = side // 2
    half_scratch = pltpu.VMEM((cut * line_slots, half), bf16)
    sofar = on_chip(
        lambda *refs: gather_kernel(0, *refs),
        jax.ShapeDtypeStruct((line_tokens, half), f32),
        (taking, *(back[s] for s in steps[:cut])),
        (half_scratch,),
    )
    weighted = on_chip(
        lambda *refs: combine_kernel(cut, *refs),
        jax.ShapeDtypeStruct((side, token_count, half), bf16),
        (taking, sofar, *(back[s] for s in steps[cut:])),
        (half_scratch,),
    )
    shares = lax.all_to_all(
        weighted, pair, 0, 0, axis_index_groups=first_groups(side), tiled=True
    )
    moe_out = jnp.sum(shares.astype(f32), axis=0).astype(bf16)
    return (moe_out, attn_latent)


def solution(mesh):
    return jax.shard_map(
        local,
        mesh=mesh,
        in_specs=(
            P(("groups", "ep"), "tp"),
            P(("groups", "ep"), None),
            P("tp", None),
            P("ep", None, "tp"),
            P("ep", None, "tp"),
            P("ep", "tp", None),
            P(("groups", "ep"), "tp", None),
            P(("groups", "ep"), "tp", None),
            P(("groups", "ep"), None, None),
            P(("groups", "ep"), None, None),
            P(("groups", "ep")),
        ),
        out_specs=(P(("groups", "ep"), "tp"), P(("groups", "ep"), "tp", None)),
        check_vma=False,
    )
```

profile of v0, /device:TPU:514, one launch (start us, length us, event | category | flops | bytes accessed | tf_op | source)
XLA Modules:
  0.0 125.4 jit_solution(6207018772005042504)
XLA Ops:
  0.6 1.2 fusion.22.own_ref
  3.9 1.7 %shard_map.122 = bf16[8,16,1920]{2,1,0:T(8,128)(2,1)} custom-call(s32[3]{0:T(128)S(1)} %pad_add_fusion.place_ref.refs_0_, bf16[16,1792]{1,0:T(8,128)(2,1)S(1)} %copy-done.1, f32[16,64]{1,0:T(8,128)S(1)} %fusion.22.own_ref, f32[16,64]{1,0:T(8,128)S(1)} %collective-permute-done.other_ref, f32[16,64]{1,0:T(8,128)S(1)} %convert_reduce_fusion.mask_ref), custom_call_target="tpu_custom_call" | custom-call | tf_op jit(solution)/shard_map/pallas_call | solution.py:52
  5.5 22.8 %all-to-all-start = ((bf16[8,16,1920]{2,1,0:T(8,128)(2,1)}), bf16[8,16,1920]{2,1,0:T(8,128)(2,1)S(1)}, u32[]{:S(2)}, u32[]{:S(2)}) async-start(bf16[8,16,1920]{2,1,0:T(8,128)(2,1)} %shard_map.122), calls=%async_computation | async-start | bytes 983040 | tf_op jit(solution)/shard_map/all_to_all | solution.py:326
  28.3 14.4 %all-to-all-done.line_ref = bf16[8,16,1920]{2,1,0:T(8,128)(2,1)S(1)} async-done(((bf16[8,16,1920]{2,1,0:T(8,128)(2,1)}), bf16[8,16,1920]{2,1,0:T(8,128)(2,1)S(1)}, u32[]{:S(2)}, u32[]{:S(2)}) %all-to-all-start) | async-done | bytes 491552 | tf_op jit(solution)/shard_map/all_to_all | solution.py:326
  44.0 5.0 %collective-permute-start.3 = (bf16[64,1792]{1,0:T(8,128)(2,1)S(1)}, bf16[64,1792]{1,0:T(8,128)(2,1)S(1)}, u32[]{:S(2)}, u32[]{:S(2)}) collective-permute-start(bf16[64,1792]{1,0:T(8,128)(2,1)S(1)} %get-tuple-element.43), channel_id=1, source_target_pairs={{0,80},{16,96},{32,112},{48,0},{64,16},{80,32},{96,48},{112,64},{2... | collective-permute-start | bytes 688136 | tf_op jit(solution)/shard_map/ppermute | solution.py:44
  49.0 4.1 %collective-permute-start.5 = (bf16[64,1792]{1,0:T(8,128)(2,1)S(1)}, bf16[64,1792]{1,0:T(8,128)(2,1)S(1)}, u32[]{:S(2)}, u32[]{:S(2)}) collective-permute-start(bf16[64,1792]{1,0:T(8,128)(2,1)S(1)} %get-tuple-element.45), channel_id=1, source_target_pairs={{0,96},{16,112},{32,0},{48,16},{64,32},{80,48},{96,64},{112,80},{2... | collective-permute-start | bytes 688136 | tf_op jit(solution)/shard_map/ppermute | solution.py:44
  53.2 4.2 %fetch_weights.1 = (bf16[3584,512]{1,0:T(8,128)(2,1)S(1)}, bf16[3584,512]{1,0:T(8,128)(2,1)S(1)}, bf16[512,3584]{1,0:T(8,128)(2,1)S(1)}, bf16[256,512]{1,0:T(8,128)(2,1)S(1)}) custom-call(bf16[3584,512]{1,0:T(8,128)(2,1)} %bitcast.19, bf16[3584,512]{1,0:T(8,128)(2,1)} %bitcast.20, bf16[512,3584]{1,0:T(8,128)(2,1)} %bitcast.21, s32[128,8]{1,0:T(8,128)S(1)} %fusion.7.refs_3_, ...), custom_call_target="tpu_custom_call" | custom-call | tf_op jit(solution)/shard_map/fetch_weights/pallas_call | solution.py:119
  57.5 1.4 %collective-permute-start.6 = (bf16[64,1792]{1,0:T(8,128)(2,1)S(1)}, bf16[64,1792]{1,0:T(8,128)(2,1)S(1)}, u32[]{:S(2)}, u32[]{:S(2)}) collective-permute-start(bf16[64,1792]{1,0:T(8,128)(2,1)S(1)} %get-tuple-element.46), channel_id=1, source_target_pairs={{0,16},{16,32},{32,48},{48,64},{64,80},{80,96},{96,112},{112,0},{2... | collective-permute-start | bytes 688136 | tf_op jit(solution)/shard_map/ppermute | solution.py:44
  58.9 1.9 %collective-permute-start.7 = (bf16[64,1792]{1,0:T(8,128)(2,1)S(1)}, bf16[64,1792]{1,0:T(8,128)(2,1)S(1)}, u32[]{:S(2)}, u32[]{:S(2)}) collective-permute-start(bf16[64,1792]{1,0:T(8,128)(2,1)S(1)} %get-tuple-element.47), channel_id=1, source_target_pairs={{0,112},{16,0},{32,16},{48,32},{64,48},{80,64},{96,80},{112,96},{2... | collective-permute-start | bytes 688136 | tf_op jit(solution)/shard_map/ppermute | solution.py:44
  62.0 2.8 %collective-permute-done.6.refs_9_ = bf16[64,1792]{1,0:T(8,128)(2,1)S(1)} collective-permute-done((bf16[64,1792]{1,0:T(8,128)(2,1)S(1)}, bf16[64,1792]{1,0:T(8,128)(2,1)S(1)}, u32[]{:S(2)}, u32[]{:S(2)}) %collective-permute-start.6) | collective-permute-done | bytes 229408 | tf_op jit(solution)/shard_map/ppermute | solution.py:44
  67.6 5.0 %shard_map.124 = (bf16[512,512]{1,0:T(8,128)(2,1)S(1)}, bf16[3,64,1792]{2,1,0:T(8,128)(2,1)S(1)}) custom-call(s32[3]{0:T(128)S(1)} %pad_add_fusion.place_ref.refs_0_, bf16[3584,512]{1,0:T(8,128)(2,1)S(1)} %get-tuple-element.38.refs_1_, bf16[3584,512]{1,0:T(8,128)(2,1)S(1)} %get-tuple-element.39.refs_2_, ...), custom_call_target="tpu_custom_call" | custom-call | tf_op jit(solution)/shard_map/pallas_call | solution.py:52
  72.6 1.3 %shard_map.126 = bf16[5,64,1792]{2,1,0:T(8,128)(2,1)S(1)} custom-call(s32[3]{0:T(128)S(1)} %pad_add_fusion.place_ref.refs_0_, bf16[512,512]{1,0:T(8,128)(2,1)S(1)} %get-tuple-element.48.refs_1_, bf16[512,3584]{1,0:T(8,128)(2,1)S(1)} %get-tuple-element.40.refs_3_.refs_2_), custom_call_target="tpu_custom_call" | custom-call | tf_op jit(solution)/shard_map/pallas_call | solution.py:52
  74.6 3.3 %collective-permute-done.16.refs_3_ = bf16[3,64,1792]{2,1,0:T(8,128)(2,1)S(1)} collective-permute-done((bf16[3,64,1792]{2,1,0:T(8,128)(2,1)S(1)}, bf16[3,64,1792]{2,1,0:T(8,128)(2,1)S(1)}, u32[]{:S(2)}, u32[]{:S(2)}) %collective-permute-start.16) | collective-permute-done | bytes 688160 | tf_op jit(solution)/shard_map/ppermute | solution.py:48
  79.0 5.9 %collective-permute-start.17 = (bf16[64,1792]{1,0:T(8,128)(2,1)S(1)}, bf16[64,1792]{1,0:T(8,128)(2,1)S(1)}, u32[]{:S(2)}, u32[]{:S(2)}) collective-permute-start(bf16[64,1792]{1,0:T(8,128)(2,1)S(1)} %get-tuple-element.50), channel_id=1, source_target_pairs={{0,64},{16,80},{32,96},{48,112},{64,0},{80,16},{96,32},{112,48},{2... | collective-permute-start | bytes 688136 | tf_op jit(solution)/shard_map/ppermute | solution.py:44
  84.9 3.8 %collective-permute-start.19 = (bf16[64,1792]{1,0:T(8,128)(2,1)S(1)}, bf16[64,1792]{1,0:T(8,128)(2,1)S(1)}, u32[]{:S(2)}, u32[]{:S(2)}) collective-permute-start(bf16[64,1792]{1,0:T(8,128)(2,1)S(1)} %get-tuple-element.52), channel_id=1, source_target_pairs={{0,48},{16,64},{32,80},{48,96},{64,112},{80,0},{96,16},{112,32},{2... | collective-permute-start | bytes 688136 | tf_op jit(solution)/shard_map/ppermute | solution.py:44
  88.7 1.3 %shard_map.127 = (bf16[64,1792]{1,0:T(8,128)(2,1)S(1)}, bf16[64,1792]{1,0:T(8,128)(2,1)S(1)}, bf16[64,1792]{1,0:T(8,128)(2,1)S(1)}, bf16[64,1792]{1,0:T(8,128)(2,1)S(1)}, bf16[64,1792]{1,0:T(8,128)(2,1)S(1)}) custom-call(s32[3]{0:T(128)S(1)} %pad_add_fusion.place_ref.refs_0_, bf16[512,512]{1,0:T(8,128)(2,1)S(1)} %get-tuple-element.48.refs_1_, ...), custom_call_target="tpu_custom_call" | custom-call | tf_op jit(solution)/shard_map/pallas_call | solution.py:52
  90.1 2.5 %collective-permute-start.21 = (bf16[64,1792]{1,0:T(8,128)(2,1)S(1)}, bf16[64,1792]{1,0:T(8,128)(2,1)S(1)}, u32[]{:S(2)}, u32[]{:S(2)}) collective-permute-start(bf16[64,1792]{1,0:T(8,128)(2,1)S(1)} %get-tuple-element.53), channel_id=1, source_target_pairs={{0,96},{16,112},{32,0},{48,16},{64,32},{80,48},{96,64},{112,80},{2... | collective-permute-start | bytes 688136 | tf_op jit(solution)/shard_map/ppermute | solution.py:44
  93.1 5.3 %collective-permute-start.23 = (bf16[64,1792]{1,0:T(8,128)(2,1)S(1)}, bf16[64,1792]{1,0:T(8,128)(2,1)S(1)}, u32[]{:S(2)}, u32[]{:S(2)}) collective-permute-start(bf16[64,1792]{1,0:T(8,128)(2,1)S(1)} %get-tuple-element.55), channel_id=1, source_target_pairs={{0,112},{16,0},{32,16},{48,32},{64,48},{80,64},{96,80},{112,96},{2... | collective-permute-start | bytes 688136 | tf_op jit(solution)/shard_map/ppermute | solution.py:44
  98.4 2.2 %collective-permute-start.24 = (bf16[64,1792]{1,0:T(8,128)(2,1)S(1)}, bf16[64,1792]{1,0:T(8,128)(2,1)S(1)}, u32[]{:S(2)}, u32[]{:S(2)}) collective-permute-start(bf16[64,1792]{1,0:T(8,128)(2,1)S(1)} %get-tuple-element.56), channel_id=1, source_target_pairs={{0,16},{16,32},{32,48},{48,64},{64,80},{80,96},{96,112},{112,0},{2... | collective-permute-start | bytes 688136 | tf_op jit(solution)/shard_map/ppermute | solution.py:44
  101.0 4.1 %collective-permute-done.21.refs_4_ = bf16[64,1792]{1,0:T(8,128)(2,1)S(1)} collective-permute-done((bf16[64,1792]{1,0:T(8,128)(2,1)S(1)}, bf16[64,1792]{1,0:T(8,128)(2,1)S(1)}, u32[]{:S(2)}, u32[]{:S(2)}) %collective-permute-start.21) | collective-permute-done | bytes 229408 | tf_op jit(solution)/shard_map/ppermute | solution.py:44
  106.7 2.3 %collective-permute-done.24.refs_4_ = bf16[64,1792]{1,0:T(8,128)(2,1)S(1)} collective-permute-done((bf16[64,1792]{1,0:T(8,128)(2,1)S(1)}, bf16[64,1792]{1,0:T(8,128)(2,1)S(1)}, u32[]{:S(2)}, u32[]{:S(2)}) %collective-permute-start.24) | collective-permute-done | bytes 229408 | tf_op jit(solution)/shard_map/ppermute | solution.py:44
  109.0 1.2 shard_map.129
  110.2 3.6 %all-to-all-start.1 = ((bf16[8,16,1792]{2,1,0:T(8,128)(2,1)}), bf16[8,16,1792]{2,1,0:T(8,128)(2,1)S(1)}, u32[]{:S(2)}, u32[]{:S(2)}) async-start(bf16[8,16,1792]{2,1,0:T(8,128)(2,1)} %shard_map.129), calls=%async_computation.1 | async-start | bytes 917504 | tf_op jit(solution)/shard_map/all_to_all | solution.py:403
  115.2 9.5 %all-to-all-done.1 = bf16[8,16,1792]{2,1,0:T(8,128)(2,1)S(1)} async-done(((bf16[8,16,1792]{2,1,0:T(8,128)(2,1)}), bf16[8,16,1792]{2,1,0:T(8,128)(2,1)S(1)}, u32[]{:S(2)}, u32[]{:S(2)}) %all-to-all-start.1) | async-done | bytes 458784 | tf_op jit(solution)/shard_map/all_to_all | solution.py:403
  (65 shorter events, 13.6 us)
Async XLA Ops:
  5.5 37.2 %all-to-all-start = ((bf16[8,16,1920]{2,1,0:T(8,128)(2,1)}), bf16[8,16,1920]{2,1,0:T(8,128)(2,1)S(1)}, u32[]{:S(2)}, u32[]{:S(2)}) async-start(bf16[8,16,1920]{2,1,0:T(8,128)(2,1)} %shard_map.122), calls=%async_computation | async-start | bytes 983040 | tf_op jit(solution)/shard_map/all_to_all | solution.py:326
  43.7 13.8 %collective-permute-start.1 = (bf16[64,1792]{1,0:T(8,128)(2,1)S(1)}, bf16[64,1792]{1,0:T(8,128)(2,1)S(1)}, u32[]{:S(2)}, u32[]{:S(2)}) collective-permute-start(bf16[64,1792]{1,0:T(8,128)(2,1)S(1)} %get-tuple-element.34), channel_id=1, source_target_pairs={{0,64},{16,80},{32,96},{48,112},{64,0},{80,16},{96,32},{112,48},{2... | collective-permute-start | bytes 688136 | tf_op jit(solution)/shard_map/ppermute | solution.py:44
  43.8 15.1 %collective-permute-start.2 = (bf16[64,1792]{1,0:T(8,128)(2,1)S(1)}, bf16[64,1792]{1,0:T(8,128)(2,1)S(1)}, u32[]{:S(2)}, u32[]{:S(2)}) collective-permute-start(bf16[64,1792]{1,0:T(8,128)(2,1)S(1)} %get-tuple-element.42), channel_id=1, source_target_pairs={{0,48},{16,64},{32,80},{48,96},{64,112},{80,0},{96,16},{112,32},{2... | collective-permute-start | bytes 688136 | tf_op jit(solution)/shard_map/ppermute | solution.py:44
  44.0 16.8 %collective-permute-start.3 = (bf16[64,1792]{1,0:T(8,128)(2,1)S(1)}, bf16[64,1792]{1,0:T(8,128)(2,1)S(1)}, u32[]{:S(2)}, u32[]{:S(2)}) collective-permute-start(bf16[64,1792]{1,0:T(8,128)(2,1)S(1)} %get-tuple-element.43), channel_id=1, source_target_pairs={{0,80},{16,96},{32,112},{48,0},{64,16},{80,32},{96,48},{112,64},{2... | collective-permute-start | bytes 688136 | tf_op jit(solution)/shard_map/ppermute | solution.py:44
  49.0 12.5 %collective-permute-start.4 = (bf16[64,1792]{1,0:T(8,128)(2,1)S(1)}, bf16[64,1792]{1,0:T(8,128)(2,1)S(1)}, u32[]{:S(2)}, u32[]{:S(2)}) collective-permute-start(bf16[64,1792]{1,0:T(8,128)(2,1)S(1)} %get-tuple-element.44), channel_id=1, source_target_pairs={{0,32},{16,48},{32,64},{48,80},{64,96},{80,112},{96,0},{112,16},{2... | collective-permute-start | bytes 688136 | tf_op jit(solution)/shard_map/ppermute | solution.py:44
  49.0 12.8 %collective-permute-start.5 = (bf16[64,1792]{1,0:T(8,128)(2,1)S(1)}, bf16[64,1792]{1,0:T(8,128)(2,1)S(1)}, u32[]{:S(2)}, u32[]{:S(2)}) collective-permute-start(bf16[64,1792]{1,0:T(8,128)(2,1)S(1)} %get-tuple-element.45), channel_id=1, source_target_pairs={{0,96},{16,112},{32,0},{48,16},{64,32},{80,48},{96,64},{112,80},{2... | collective-permute-start | bytes 688136 | tf_op jit(solution)/shard_map/ppermute | solution.py:44
  57.5 7.3 %collective-permute-start.6 = (bf16[64,1792]{1,0:T(8,128)(2,1)S(1)}, bf16[64,1792]{1,0:T(8,128)(2,1)S(1)}, u32[]{:S(2)}, u32[]{:S(2)}) collective-permute-start(bf16[64,1792]{1,0:T(8,128)(2,1)S(1)} %get-tuple-element.46), channel_id=1, source_target_pairs={{0,16},{16,32},{32,48},{48,64},{64,80},{80,96},{96,112},{112,0},{2... | collective-permute-start | bytes 688136 | tf_op jit(solution)/shard_map/ppermute | solution.py:44
  58.9 6.0 %collective-permute-start.7 = (bf16[64,1792]{1,0:T(8,128)(2,1)S(1)}, bf16[64,1792]{1,0:T(8,128)(2,1)S(1)}, u32[]{:S(2)}, u32[]{:S(2)}) collective-permute-start(bf16[64,1792]{1,0:T(8,128)(2,1)S(1)} %get-tuple-element.47), channel_id=1, source_target_pairs={{0,112},{16,0},{32,16},{48,32},{64,48},{80,64},{96,80},{112,96},{2... | collective-permute-start | bytes 688136 | tf_op jit(solution)/shard_map/ppermute | solution.py:44
  60.8 4.5 %collective-permute-start.15 = (bf16[64,1792]{1,0:T(8,128)(2,1)S(1)}, bf16[64,1792]{1,0:T(8,128)(2,1)S(1)}, u32[]{:S(2)}, u32[]{:S(2)}) collective-permute-start(bf16[64,1792]{1,0:T(8,128)(2,1)S(1)} %get-tuple-element.31.refs_6_.refs_11_), channel_id=1, source_target_pairs={{0,1},{1,0},{2,3},{3,2},{4,5},{5,4},{6,7},{7,6},{8,9},{9,8},{10,11... | collective-permute-start | bytes 688136 | tf_op jit(solution)/shard_map/ppermute | solution.py:48
  61.5 4.0 %collective-permute-start.8 = (bf16[64,1792]{1,0:T(8,128)(2,1)S(1)}, bf16[64,1792]{1,0:T(8,128)(2,1)S(1)}, u32[]{:S(2)}, u32[]{:S(2)}) collective-permute-start(bf16[64,1792]{1,0:T(8,128)(2,1)S(1)} %collective-permute-done.1.refs_4_), channel_id=1, source_target_pairs={{0,1},{1,0},{2,3},{3,2},{4,5},{5,4},{6,7},{7,6},{8,9},{9,8},{10,11... | collective-permute-start | bytes 688136 | tf_op jit(solution)/shard_map/ppermute | solution.py:48
  61.8 4.1 %collective-permute-start.9 = (bf16[64,1792]{1,0:T(8,128)(2,1)S(1)}, bf16[64,1792]{1,0:T(8,128)(2,1)S(1)}, u32[]{:S(2)}, u32[]{:S(2)}) collective-permute-start(bf16[64,1792]{1,0:T(8,128)(2,1)S(1)} %collective-permute-done.2.refs_5_), channel_id=1, source_target_pairs={{0,1},{1,0},{2,3},{3,2},{4,5},{5,4},{6,7},{7,6},{8,9},{9,8},{10,11... | collective-permute-start | bytes 688136 | tf_op jit(solution)/shard_map/ppermute | solution.py:48
  64.9 1.7 %collective-permute-start.11 = (bf16[64,1792]{1,0:T(8,128)(2,1)S(1)}, bf16[64,1792]{1,0:T(8,128)(2,1)S(1)}, u32[]{:S(2)}, u32[]{:S(2)}) collective-permute-start(bf16[64,1792]{1,0:T(8,128)(2,1)S(1)} %collective-permute-done.4.refs_7_), channel_id=1, source_target_pairs={{0,1},{1,0},{2,3},{3,2},{4,5},{5,4},{6,7},{7,6},{8,9},{9,8},{10,11... | collective-permute-start | bytes 688136 | tf_op jit(solution)/shard_map/ppermute | solution.py:48
  65.5 1.8 %collective-permute-start.13 = (bf16[64,1792]{1,0:T(8,128)(2,1)S(1)}, bf16[64,1792]{1,0:T(8,128)(2,1)S(1)}, u32[]{:S(2)}, u32[]{:S(2)}) collective-permute-start(bf16[64,1792]{1,0:T(8,128)(2,1)S(1)} %collective-permute-done.6.refs_9_), channel_id=1, source_target_pairs={{0,1},{1,0},{2,3},{3,2},{4,5},{5,4},{6,7},{7,6},{8,9},{9,8},{10,11... | collective-permute-start | bytes 688136 | tf_op jit(solution)/shard_map/ppermute | solution.py:48
  65.8 1.8 %collective-permute-start.14 = (bf16[64,1792]{1,0:T(8,128)(2,1)S(1)}, bf16[64,1792]{1,0:T(8,128)(2,1)S(1)}, u32[]{:S(2)}, u32[]{:S(2)}) collective-permute-start(bf16[64,1792]{1,0:T(8,128)(2,1)S(1)} %collective-permute-done.7.refs_10_), channel_id=1, source_target_pairs={{0,1},{1,0},{2,3},{3,2},{4,5},{5,4},{6,7},{7,6},{8,9},{9,8},{10,11... | collective-permute-start | bytes 688136 | tf_op jit(solution)/shard_map/ppermute | solution.py:48
  73.9 14.8 %collective-permute-start.20 = (bf16[5,64,1792]{2,1,0:T(8,128)(2,1)S(1)}, bf16[5,64,1792]{2,1,0:T(8,128)(2,1)S(1)}, u32[]{:S(2)}, u32[]{:S(2)}) collective-permute-start(bf16[5,64,1792]{2,1,0:T(8,128)(2,1)S(1)} %shard_map.126), channel_id=1, source_target_pairs={{0,1},{1,0},{2,3},{3,2},{4,5},{5,4},{6,7},{7,6},{8,9},{9,8},{10,11... | collective-permute-start | bytes 3440648 | tf_op jit(solution)/shard_map/ppermute | solution.py:48
  74.3 3.6 %collective-permute-start.16 = (bf16[3,64,1792]{2,1,0:T(8,128)(2,1)S(1)}, bf16[3,64,1792]{2,1,0:T(8,128)(2,1)S(1)}, u32[]{:S(2)}, u32[]{:S(2)}) collective-permute-start(bf16[3,64,1792]{2,1,0:T(8,128)(2,1)S(1)} %get-tuple-element.49), channel_id=1, source_target_pairs={{0,1},{1,0},{2,3},{3,2},{4,5},{5,4},{6,7},{7,6},{8,9},{9,8},{10,11... | collective-permute-start | bytes 2064392 | tf_op jit(solution)/shard_map/ppermute | solution.py:48
  79.0 14.2 %collective-permute-start.17 = (bf16[64,1792]{1,0:T(8,128)(2,1)S(1)}, bf16[64,1792]{1,0:T(8,128)(2,1)S(1)}, u32[]{:S(2)}, u32[]{:S(2)}) collective-permute-start(bf16[64,1792]{1,0:T(8,128)(2,1)S(1)} %get-tuple-element.50), channel_id=1, source_target_pairs={{0,64},{16,80},{32,96},{48,112},{64,0},{80,16},{96,32},{112,48},{2... | collective-permute-start | bytes 688136 | tf_op jit(solution)/shard_map/ppermute | solution.py:44
  84.9 13.6 %collective-permute-start.18 = (bf16[64,1792]{1,0:T(8,128)(2,1)S(1)}, bf16[64,1792]{1,0:T(8,128)(2,1)S(1)}, u32[]{:S(2)}, u32[]{:S(2)}) collective-permute-start(bf16[64,1792]{1,0:T(8,128)(2,1)S(1)} %get-tuple-element.51), channel_id=1, source_target_pairs={{0,80},{16,96},{32,112},{48,0},{64,16},{80,32},{96,48},{112,64},{2... | collective-permute-start | bytes 688136 | tf_op jit(solution)/shard_map/ppermute | solution.py:44
  84.9 16.1 %collective-permute-start.19 = (bf16[64,1792]{1,0:T(8,128)(2,1)S(1)}, bf16[64,1792]{1,0:T(8,128)(2,1)S(1)}, u32[]{:S(2)}, u32[]{:S(2)}) collective-permute-start(bf16[64,1792]{1,0:T(8,128)(2,1)S(1)} %get-tuple-element.52), channel_id=1, source_target_pairs={{0,48},{16,64},{32,80},{48,96},{64,112},{80,0},{96,16},{112,32},{2... | collective-permute-start | bytes 688136 | tf_op jit(solution)/shard_map/ppermute | solution.py:44
  90.1 15.0 %collective-permute-start.21 = (bf16[64,1792]{1,0:T(8,128)(2,1)S(1)}, bf16[64,1792]{1,0:T(8,128)(2,1)S(1)}, u32[]{:S(2)}, u32[]{:S(2)}) collective-permute-start(bf16[64,1792]{1,0:T(8,128)(2,1)S(1)} %get-tuple-element.53), channel_id=1, source_target_pairs={{0,96},{16,112},{32,0},{48,16},{64,32},{80,48},{96,64},{112,80},{2... | collective-permute-start | bytes 688136 | tf_op jit(solution)/shard_map/ppermute | solution.py:44
  92.5 13.0 %collective-permute-start.22 = (bf16[64,1792]{1,0:T(8,128)(2,1)S(1)}, bf16[64,1792]{1,0:T(8,128)(2,1)S(1)}, u32[]{:S(2)}, u32[]{:S(2)}) collective-permute-start(bf16[64,1792]{1,0:T(8,128)(2,1)S(1)} %get-tuple-element.54), channel_id=1, source_target_pairs={{0,32},{16,48},{32,64},{48,80},{64,96},{80,112},{96,0},{112,16},{2... | collective-permute-start | bytes 688136 | tf_op jit(solution)/shard_map/ppermute | solution.py:44
  93.1 13.6 %collective-permute-start.23 = (bf16[64,1792]{1,0:T(8,128)(2,1)S(1)}, bf16[64,1792]{1,0:T(8,128)(2,1)S(1)}, u32[]{:S(2)}, u32[]{:S(2)}) collective-permute-start(bf16[64,1792]{1,0:T(8,128)(2,1)S(1)} %get-tuple-element.55), channel_id=1, source_target_pairs={{0,112},{16,0},{32,16},{48,32},{64,48},{80,64},{96,80},{112,96},{2... | collective-permute-start | bytes 688136 | tf_op jit(solution)/shard_map/ppermute | solution.py:44
  98.4 10.6 %collective-permute-start.24 = (bf16[64,1792]{1,0:T(8,128)(2,1)S(1)}, bf16[64,1792]{1,0:T(8,128)(2,1)S(1)}, u32[]{:S(2)}, u32[]{:S(2)}) collective-permute-start(bf16[64,1792]{1,0:T(8,128)(2,1)S(1)} %get-tuple-element.56), channel_id=1, source_target_pairs={{0,16},{16,32},{32,48},{48,64},{64,80},{80,96},{96,112},{112,0},{2... | collective-permute-start | bytes 688136 | tf_op jit(solution)/shard_map/ppermute | solution.py:44
  110.2 14.4 %all-to-all-start.1 = ((bf16[8,16,1792]{2,1,0:T(8,128)(2,1)}), bf16[8,16,1792]{2,1,0:T(8,128)(2,1)S(1)}, u32[]{:S(2)}, u32[]{:S(2)}) async-start(bf16[8,16,1792]{2,1,0:T(8,128)(2,1)} %shard_map.129), calls=%async_computation.1 | async-start | bytes 917504 | tf_op jit(solution)/shard_map/all_to_all | solution.py:403
  (9 other events, 198.2 us)
where the time goes:
time: 126 us; the launch traced here: 125 us
  starting transfers between devices  61.5 us (49%)
  waiting for transfers between devices  40.3 us (32%)
  Pallas kernels  16.9 us (13%)
  matrix products  2.93 us (2%)
  other arithmetic  1.89 us (2%)
    ppermute x14, starting transfers between devices, shifted(): return lax.ppermute(value, pair, moves)  33 us
    all_to_all x1, starting transfers between devices, local(): lax.all_to_all(message, pair, 0, 0, axis_index_groups=first_groups(side),...  22.8 us
    all_to_all x1, waiting for transfers between devices, local(): lax.all_to_all(message, pair, 0, 0, axis_index_groups=first_groups(side),...  14.4 us
    pallas_call x8, Pallas kernels, on_chip(): pl.pallas_call(kernel, out_shape=out_shapes, in_specs=[pl.BlockSpec(memor...  12.6 us
    ppermute x14, waiting for transfers between devices, shifted(): return lax.ppermute(value, pair, moves)  11.5 us
    all_to_all x1, waiting for transfers between devices, local(): lax.all_to_all(weighted, pair, 0, 0, axis_index_groups=first_groups(side)...  9.47 us
    ppermute x11, waiting for transfers between devices, swapped(): return lax.ppermute(value, axis, [(0, 1), (1, 0)])  4.98 us
    pallas_call x1, Pallas kernels, fetched(): pl.pallas_call(fetch_kernel, out_shape=tuple((pltpu.VMEM(a.shape, a.dtype...  4.23 us
  transfers between devices with their start and end apart: 27, of which 16 were waited for; matrix products, arithmetic and copies ran while one was open for 2% of the time, Pallas kernels for 6%

commit v1 on v0

--- a/solution.py
+++ b/solution.py
@@ -61,48 +61,53 @@
     )(*operands)
 
 
-def message_kernel(place_ref, hidden_ref, own_ref, other_ref, mask_ref, message_ref):
+def message_kernel(place_ref, hidden_ref, own_ref, other_ref, mask_ref, message_ref, sum_ref):
     side, _, width = message_ref.shape
     half = hidden_ref.shape[1]
     lanes = width - half
     expert_count = mask_ref.shape[1]
     core, second = place_ref[1], place_ref[2]
     chosen = jnp.where(mask_ref[...] > 0, jax.nn.sigmoid(own_ref[...] + other_ref[...]), 0.0)
-    gates = routed_scale * chosen / jnp.sum(chosen, axis=1, keepdims=True)
+    affinity_sum = jnp.sum(chosen, axis=1, keepdims=True)
+    sum_ref[...] = affinity_sum
+    gates = jnp.where(affinity_sum > 0, routed_scale * chosen / affinity_sum, 0.0)
     parts = jnp.concatenate([part.astype(jnp.float32) for part in split_in_two(gates)], axis=1)
-    shape = (2 * expert_count, lanes)
+    shape = (2 * expert_count, side * lanes)
     source = lax.broadcasted_iota(jnp.int32, shape, 0)
-    lane = lax.broadcasted_iota(jnp.int32, shape, 1)
+    column = lax.broadcasted_iota(jnp.int32, shape, 1)
+    first = lax.div(column, lanes)
+    lane = column - first * lanes
     low = (lane >= side).astype(jnp.int32)
     ahead = lax.rem(lane - low * side + second, side)
-    scale = jnp.where(core == 0, side, 1)
-    base = ahead * scale + low * expert_count
+    wanted = jnp.where(core == 0, ahead * side + first, first * side + ahead) + low * expert_count
+    select = jnp.where((lane < 2 * side) & (wanted == source), 1.0, 0.0).astype(jnp.bfloat16)
+    picked = jnp.dot(parts.astype(jnp.bfloat16), select, preferred_element_type=jnp.float32)
+    picked = picked.astype(jnp.bfloat16)
     for first in range(side):
-        wanted = base + first * jnp.where(core == 0, 1, side)
-        select = jnp.where((lane < 2 * side) & (wanted == source), 1.0, 0.0)
-        picked = jnp.dot(
-            parts.astype(jnp.bfloat16), select.astype(jnp.bfloat16), preferred_element_type=jnp.float32
-        )
         message_ref[first, :, pl.ds(0, half)] = hidden_ref[...]
-        message_ref[first, :, pl.ds(half, lanes)] = picked.astype(jnp.bfloat16)
-
-
-def fetch_kernel(*refs):
-    sources, (slot_ref, high_ref, low_ref, _), refs = refs[:3], refs[3:7], refs[7:]
+        message_ref[first, :, pl.ds(half, lanes)] = picked[:, first * lanes : (first + 1) * lanes]
+
+
+def fetch_kernel(side, *refs):
+    sources, (slot_ref, gate_ref, _), refs = refs[:3], refs[3:6], refs[6:]
     targets, taking, sems = refs[:3], refs[3], refs[4:]
     copies = [pltpu.make_async_copy(s, t, m) for s, t, m in zip(sources, targets, sems)]
     for copy in copies:
         copy.start()
-    line_tokens, side = slot_ref.shape
+    line_tokens = slot_ref.shape[0]
     slots = taking.shape[1] // side
     slot_iota = lax.broadcasted_iota(jnp.int32, (line_tokens, slots), 1)
     steps = far_to_near(side)
     for place in range(0, side, 2):
         columns = pl.ds(place * slots, 2 * slots)
         pair_of = steps[place : place + 2]
-        for index, part_ref in enumerate((high_ref, low_ref)):
+        for index in range(2):
             taken = [
-                jnp.where(slot_ref[:, s : s + 1] == slot_iota, part_ref[:, s : s + 1], 0.0)
+                jnp.where(
+                    slot_ref[:, s : s + 1] == slot_iota,
+                    gate_ref[:, index * side + s : index * side + s + 1],
+                    0.0,
+                )
                 for s in pair_of
             ]
             taking[pl.ds(index * line_tokens, line_tokens), columns] = jnp.concatenate(
@@ -112,32 +117,50 @@
         copy.wait()
 
 
-def fetched(arrays, slot, high, low, after):
-    line_tokens, side = slot.shape
+def fetched(arrays, side, slot, gates, after):
+    line_tokens = slot.shape[0]
     taking_shape = (2 * line_tokens, side * after.shape[0])
     vmem = pl.BlockSpec(memory_space=pltpu.VMEM)
     return pl.pallas_call(
-        fetch_kernel,
+        lambda *refs: fetch_kernel(side, *refs),
         out_shape=tuple(pltpu.VMEM(a.shape, a.dtype) for a in arrays)
         + (jax.ShapeDtypeStruct(taking_shape, jnp.bfloat16),),
         in_specs=[pl.BlockSpec(memory_space=pltpu.HBM)] * 3
-        + [vmem] * 3
+        + [vmem] * 2
         + [pl.BlockSpec(memory_space=pl.ANY)],
         out_specs=(vmem,) * 4,
         scratch_shapes=[pltpu.SemaphoreType.DMA] * len(arrays),
         compiler_params=pltpu.CompilerParams(vmem_limit_bytes=42 * 1024 * 1024),
         name="fetch_weights",
-    )(*arrays, slot, high, low, after)
-
-
-def select_kernel(slot_ref, line_ref, *part_refs):
-    side, line_tokens = slot_ref.shape
+    )(*arrays, slot, gates, after)
+
+
+def select_kernel(capacity, place_ref, line_ref, *refs):
+    part_refs, (slot_ref, gate_ref) = refs[:-2], refs[-2:]
+    side, token_count, width = line_ref.shape
     slots, half = part_refs[0].shape
-    tokens = line_ref[:, :, :half].reshape(line_tokens, half)
+    line_tokens = side * token_count
+    first = place_ref[3]
+    gates = line_ref[:, :, pl.ds(half, width - half)].reshape(line_tokens, width - half)
+    gates = gates.astype(jnp.float32)
+    gate_ref[...] = gates
+    shape = (line_tokens, line_tokens)
+    later = lax.broadcasted_iota(jnp.int32, shape, 0)
+    earlier = lax.broadcasted_iota(jnp.int32, shape, 1)
+    same = lax.div(later, token_count) == lax.div(earlier, token_count)
+    before = jnp.where(same & (later > earlier), 1.0, 0.0).astype(jnp.bfloat16)
+    picked = jnp.where(gates != 0, 1.0, 0.0).astype(jnp.bfloat16)
+    rank = jnp.dot(before, picked, preferred_element_type=jnp.float32)
+    block = lax.div(lax.broadcasted_iota(jnp.int32, gates.shape, 0), token_count)
+    offset = lax.rem(first - block + side, side) * capacity
+    slot = jnp.where(gates != 0, offset.astype(jnp.float32) + rank, -1.0)
+    slot_ref[...] = slot.astype(jnp.int32)
+    slot_rows = jnp.transpose(slot).astype(jnp.int32)
+    tokens = line_ref[:, :, pl.ds(0, half)].reshape(line_tokens, half)
     slot_iota = lax.broadcasted_iota(jnp.int32, (slots, line_tokens), 0)
     for step in range(side):
-        placing = (slot_ref[step : step + 1, :] == slot_iota).astype(jnp.float32).astype(jnp.bfloat16)
-        rows = jnp.dot(placing, tokens, preferred_element_type=jnp.float32)
+        placing = jnp.where(slot_rows[step : step + 1, :] == slot_iota, 1.0, 0.0)
+        rows = jnp.dot(placing.astype(jnp.bfloat16), tokens, preferred_element_type=jnp.float32)
         part_refs[step][...] = rows.astype(jnp.bfloat16)
 
 
@@ -242,6 +265,7 @@
 
 
 def combine_kernel(place, taking_ref, sofar_ref, *refs):
+    refs = refs[1:]
     back_refs, (out_ref, rows) = refs[:-2], refs[-2:]
     slots, half = back_refs[0].shape
     depth = len(back_refs) * slots
@@ -257,6 +281,13 @@
         out_ref[:, :, columns] = total.astype(jnp.bfloat16).reshape(
             out_ref.shape[0], out_ref.shape[1], tile
         )
+
+
+def total_kernel(sum_ref, share_ref, out_ref):
+    total = share_ref[0].astype(jnp.float32)
+    for step in range(1, share_ref.shape[0]):
+        total = total + share_ref[step].astype(jnp.float32)
+    out_ref[...] = jnp.where(sum_ref[...] > 0, total, jnp.nan).astype(out_ref.dtype)
 
 
 def split_in_two(value):
@@ -309,7 +340,7 @@
     row, column = place // side, place % side
     first = jnp.where(core == 0, column, row)
     second = jnp.where(core == 0, row, column)
-    start = jnp.stack([core * half, core, second]).astype(jnp.int32)
+    start = jnp.stack([core * half, core, second, first]).astype(jnp.int32)
 
     expert_iota = jnp.arange(expert_count, dtype=jnp.int32)
     mask = jnp.sum((routes.T[:, :, None] == expert_iota).astype(f32), axis=0)
@@ -317,34 +348,34 @@
     other_logits = swapped(partial_logits, "tp")
 
     lanes = 128 * ((2 * side + 127) // 128)
-    message = on_chip(
+    message, affinity_sum = on_chip(
         message_kernel,
-        jax.ShapeDtypeStruct((side, token_count, half + lanes), bf16),
+        (
+            jax.ShapeDtypeStruct((side, token_count, half + lanes), bf16),
+            jax.ShapeDtypeStruct((token_count, 1), f32),
+        ),
         (start, hidden, partial_logits, other_logits, mask),
     )
-    message, start = lax.optimization_barrier((message, start))
     line = lax.all_to_all(
         message, pair, 0, 0, axis_index_groups=first_groups(side), tiled=True
     )
-    line_gates = line[:, :, half : half + 2 * side].reshape(line_tokens, 2 * side)
-    gate_high, gate_low = line_gates[:, :side].astype(f32), line_gates[:, side:].astype(f32)
-
-    picked = gate_high != 0
-    token_iota = jnp.arange(line_tokens, dtype=jnp.int32)
-    block_of = token_iota // token_count
-    before = (token_iota[:, None] > token_iota[None, :]) & (block_of[:, None] == block_of[None, :])
-    rank = jnp.dot(before.astype(bf16), picked.astype(bf16), preferred_element_type=f32)
-    offset = ((first - block_of + side) % side) * capacity
-    slot = jnp.where(picked, offset[:, None] + rank.astype(jnp.int32), -1)
     part_shape = jax.ShapeDtypeStruct((line_slots, half), bf16)
-    rows = on_chip(select_kernel, (part_shape,) * side, (slot.T, line))
+    *rows, slot, line_gates = on_chip(
+        lambda *refs: select_kernel(capacity, *refs),
+        (part_shape,) * side
+        + (
+            jax.ShapeDtypeStruct((line_tokens, lanes), jnp.int32),
+            jax.ShapeDtypeStruct((line_tokens, lanes), f32),
+        ),
+        (start, line),
+    )
 
     order = [step for step in far_to_near(side) if step]
     own, other = [rows[0]] + [None] * (side - 1), [None] * side
     for step in order:
         own[step] = shifted(rows[step], step, side)
     weights = (gate_weight[0], up_weight[0], down_weight[0])
-    *weights, taking = fetched(weights, slot, gate_high, gate_low, rows[0])
+    *weights, taking = fetched(weights, side, slot, line_gates, rows[0])
     other[0] = swapped(own[0], "tp")
     own[order[0]], *weights = lax.optimization_barrier((own[order[0]], *weights))
     for step in order:
@@ -397,13 +428,15 @@
     weighted = on_chip(
         lambda *refs: combine_kernel(cut, *refs),
         jax.ShapeDtypeStruct((side, token_count, half), bf16),
-        (taking, sofar, *(back[s] for s in steps[cut:])),
+        (taking, sofar, attn_latent, *(back[s] for s in steps[cut:])),
         (half_scratch,),
     )
     shares = lax.all_to_all(
         weighted, pair, 0, 0, axis_index_groups=first_groups(side), tiled=True
     )
-    moe_out = jnp.sum(shares.astype(f32), axis=0).astype(bf16)
+    moe_out = on_chip(
+        total_kernel, jax.ShapeDtypeStruct((token_count, half), bf16), (affinity_sum, shares)
+    )
     return (moe_out, attn_latent)
 
 

time: 126 us -> 122 us (0.968)
  blocking collectives: 0 us -> 48.4 us
  starting transfers between devices: 61.5 us -> 31.5 us
  waiting for transfers between devices: 40.3 us -> 18 us
    all_to_all x0 -> x2, blocking collectives: none -> 48.4 us  [the longest x1 33.6 us: local(): lax.all_to_all(message, pair, 0, 0, axis_index_groups=first_groups(side),...]
    all_to_all x2 -> x0, starting transfers between devices: 26.3 us -> none  [the longest x1 22.8 us: local(): lax.all_to_all(message, pair, 0, 0, axis_index_groups=first_groups(side),...]
    all_to_all x2 -> x0, waiting for transfers between devices: 23.9 us -> none  [the longest x1 14.4 us: local(): lax.all_to_all(message, pair, 0, 0, axis_index_groups=first_groups(side),...]
    ppermute x14, starting transfers between devices: 33 us -> 28.9 us  [shifted(): return lax.ppermute(value, pair, moves)]
    ppermute x14, waiting for transfers between devices: 11.5 us -> 13.5 us  [shifted(): return lax.ppermute(value, pair, moves)]
    pallas_call x8 -> x9, Pallas kernels: 12.6 us -> 13.3 us  [on_chip(): pl.pallas_call(kernel, out_shape=out_shapes, in_specs=[pl.BlockSpec(memor...]
  transfers between devices with their start and end apart: 27 -> 25, of which waited for: 16 -> 14; matrix products, arithmetic and copies ran while one was open for 2% -> 2% of each run, Pallas kernels for 6% -> 7%
where the time goes in v1:
time: 122 us; the launch traced here: 121 us
  blocking collectives  48.4 us (40%)
  starting transfers between devices  31.5 us (26%)
  waiting for transfers between devices  18 us (15%)
  Pallas kernels  17.6 us (14%)
  matrix products  3.03 us (2%)
    all_to_all x1, blocking collectives, local(): lax.all_to_all(message, pair, 0, 0, axis_index_groups=first_groups(side),...  33.6 us
    ppermute x14, starting transfers between devices, shifted(): return lax.ppermute(value, pair, moves)  28.9 us
    all_to_all x1, blocking collectives, local(): lax.all_to_all(weighted, pair, 0, 0, axis_index_groups=first_groups(side)...  14.8 us
    ppermute x14, waiting for transfers between devices, shifted(): return lax.ppermute(value, pair, moves)  13.5 us
    pallas_call x9, Pallas kernels, on_chip(): pl.pallas_call(kernel, out_shape=out_shapes, in_specs=[pl.BlockSpec(memor...  13.3 us
    ppermute x11, waiting for transfers between devices, swapped(): return lax.ppermute(value, axis, [(0, 1), (1, 0)])  4.51 us
    pallas_call x1, Pallas kernels, fetched(): pl.pallas_call(lambda *refs: fetch_kernel(side, *refs), out_shape=tuple((...  4.23 us
    ppermute x11, starting transfers between devices, swapped(): return lax.ppermute(value, axis, [(0, 1), (1, 0)])  2.54 us
  transfers between devices with their start and end apart: 25, of which 14 were waited for; matrix products, arithmetic and copies ran while one was open for 2% of the time, Pallas kernels for 7%

profile of v1, /device:TPU:514, one launch (start us, length us, event | category | flops | bytes accessed | tf_op | source)
XLA Modules:
  0.0 121.3 jit_solution(798202489041983790)
XLA Ops:
  0.6 1.2 fusion.10.own_ref
  4.7 33.6 %all_to_all.10.refs_1_ = bf16[8,16,1920]{2,1,0:T(8,128)(2,1)S(1)} all-to-all(bf16[8,16,1920]{2,1,0:T(8,128)(2,1)S(1)} %get-tuple-element.33), channel_id=1, replica_groups={{0,2,4,6,8,10,12,14},{16,18,20,22,24,26,28,30},{32,34,36,38,40,42,44,46..., dimensions={0} | all-to-all | bytes 983040 | tf_op jit(solution)/shard_map/all_to_all | solution.py:359
  38.3 1.4 %shard_map.123 = (bf16[64,1792]{1,0:T(8,128)(2,1)S(1)}, bf16[64,1792]{1,0:T(8,128)(2,1)S(1)}, bf16[64,1792]{1,0:T(8,128)(2,1)S(1)}, bf16[64,1792]{1,0:T(8,128)(2...) custom-call(s32[4]{0:T(128)S(1)} %pad_add_fusion.place_ref.refs_0_, ...), custom_call_target="tpu_custom_call" | custom-call | tf_op jit(solution)/shard_map/pallas_call | solution.py:52
  40.3 4.7 %collective-permute-start.3 = (bf16[64,1792]{1,0:T(8,128)(2,1)S(1)}, bf16[64,1792]{1,0:T(8,128)(2,1)S(1)}, u32[]{:S(2)}, u32[]{:S(2)}) collective-permute-start(bf16[64,1792]{1,0:T(8,128)(2,1)S(1)} %get-tuple-element.47), channel_id=1, source_target_pairs={{0,80},{16,96},{32,112},{48,0},{64,16},{80,32},{96,48},{112,64},{2... | collective-permute-start | bytes 688136 | tf_op jit(solution)/shard_map/ppermute | solution.py:44
  45.0 4.1 %collective-permute-start.5 = (bf16[64,1792]{1,0:T(8,128)(2,1)S(1)}, bf16[64,1792]{1,0:T(8,128)(2,1)S(1)}, u32[]{:S(2)}, u32[]{:S(2)}) collective-permute-start(bf16[64,1792]{1,0:T(8,128)(2,1)S(1)} %get-tuple-element.49), channel_id=1, source_target_pairs={{0,96},{16,112},{32,0},{48,16},{64,32},{80,48},{96,64},{112,80},{2... | collective-permute-start | bytes 688136 | tf_op jit(solution)/shard_map/ppermute | solution.py:44
  49.2 4.2 %fetch_weights.1 = (bf16[3584,512]{1,0:T(8,128)(2,1)S(1)}, bf16[3584,512]{1,0:T(8,128)(2,1)S(1)}, bf16[512,3584]{1,0:T(8,128)(2,1)S(1)}, bf16[256,512]{1,0:T(8,128)(2,1)S(1)}) custom-call(bf16[3584,512]{1,0:T(8,128)(2,1)} %bitcast.17, bf16[3584,512]{1,0:T(8,128)(2,1)} %bitcast.18, bf16[512,3584]{1,0:T(8,128)(2,1)} %bitcast.19, ...), custom_call_target="tpu_custom_call" | custom-call | tf_op jit(solution)/shard_map/fetch_weights/pallas_call | solution.py:124
  53.4 3.0 %collective-permute-done.1.refs_4_ = bf16[64,1792]{1,0:T(8,128)(2,1)S(1)} collective-permute-done((bf16[64,1792]{1,0:T(8,128)(2,1)S(1)}, bf16[64,1792]{1,0:T(8,128)(2,1)S(1)}, u32[]{:S(2)}, u32[]{:S(2)}) %collective-permute-start.1) | collective-permute-done | bytes 229408 | tf_op jit(solution)/shard_map/ppermute | solution.py:44
  56.4 3.2 %collective-permute-start.7 = (bf16[64,1792]{1,0:T(8,128)(2,1)S(1)}, bf16[64,1792]{1,0:T(8,128)(2,1)S(1)}, u32[]{:S(2)}, u32[]{:S(2)}) collective-permute-start(bf16[64,1792]{1,0:T(8,128)(2,1)S(1)} %get-tuple-element.51), channel_id=1, source_target_pairs={{0,112},{16,0},{32,16},{48,32},{64,48},{80,64},{96,80},{112,96},{2... | collective-permute-start | bytes 688136 | tf_op jit(solution)/shard_map/ppermute | solution.py:44
  60.3 3.3 %collective-permute-done.6.refs_9_ = bf16[64,1792]{1,0:T(8,128)(2,1)S(1)} collective-permute-done((bf16[64,1792]{1,0:T(8,128)(2,1)S(1)}, bf16[64,1792]{1,0:T(8,128)(2,1)S(1)}, u32[]{:S(2)}, u32[]{:S(2)}) %collective-permute-start.6) | collective-permute-done | bytes 229408 | tf_op jit(solution)/shard_map/ppermute | solution.py:44
  66.4 5.0 %shard_map.124 = (bf16[512,512]{1,0:T(8,128)(2,1)S(1)}, bf16[3,64,1792]{2,1,0:T(8,128)(2,1)S(1)}) custom-call(s32[4]{0:T(128)S(1)} %pad_add_fusion.place_ref.refs_0_, bf16[3584,512]{1,0:T(8,128)(2,1)S(1)} %get-tuple-element.42.refs_1_, bf16[3584,512]{1,0:T(8,128)(2,1)S(1)} %get-tuple-element.43.refs_2_, ...), custom_call_target="tpu_custom_call" | custom-call | tf_op jit(solution)/shard_map/pallas_call | solution.py:52
  71.5 1.3 %shard_map.126 = bf16[5,64,1792]{2,1,0:T(8,128)(2,1)S(1)} custom-call(s32[4]{0:T(128)S(1)} %pad_add_fusion.place_ref.refs_0_, bf16[512,512]{1,0:T(8,128)(2,1)S(1)} %get-tuple-element.52.refs_1_, bf16[512,3584]{1,0:T(8,128)(2,1)S(1)} %get-tuple-element.44.refs_3_.refs_2_), custom_call_target="tpu_custom_call" | custom-call | tf_op jit(solution)/shard_map/pallas_call | solution.py:52
  74.0 2.8 %collective-permute-done.16.refs_3_ = bf16[3,64,1792]{2,1,0:T(8,128)(2,1)S(1)} collective-permute-done((bf16[3,64,1792]{2,1,0:T(8,128)(2,1)S(1)}, bf16[3,64,1792]{2,1,0:T(8,128)(2,1)S(1)}, u32[]{:S(2)}, u32[]{:S(2)}) %collective-permute-start.16) | collective-permute-done | bytes 688160 | tf_op jit(solution)/shard_map/ppermute | solution.py:48
  76.8 1.1 shard_map.125
  77.8 4.2 %collective-permute-start.17 = (bf16[64,1792]{1,0:T(8,128)(2,1)S(1)}, bf16[64,1792]{1,0:T(8,128)(2,1)S(1)}, u32[]{:S(2)}, u32[]{:S(2)}) collective-permute-start(bf16[64,1792]{1,0:T(8,128)(2,1)S(1)} %get-tuple-element.54), channel_id=1, source_target_pairs={{0,64},{16,80},{32,96},{48,112},{64,0},{80,16},{96,32},{112,48},{2... | collective-permute-start | bytes 688136 | tf_op jit(solution)/shard_map/ppermute | solution.py:44
  82.4 3.9 %collective-permute-start.19 = (bf16[64,1792]{1,0:T(8,128)(2,1)S(1)}, bf16[64,1792]{1,0:T(8,128)(2,1)S(1)}, u32[]{:S(2)}, u32[]{:S(2)}) collective-permute-start(bf16[64,1792]{1,0:T(8,128)(2,1)S(1)} %get-tuple-element.56), channel_id=1, source_target_pairs={{0,48},{16,64},{32,80},{48,96},{64,112},{80,0},{96,16},{112,32},{2... | collective-permute-start | bytes 688136 | tf_op jit(solution)/shard_map/ppermute | solution.py:44
  86.3 2.2 %shard_map.127 = (bf16[64,1792]{1,0:T(8,128)(2,1)}, bf16[64,1792]{1,0:T(8,128)(2,1)}, bf16[64,1792]{1,0:T(8,128)(2,1)}, bf16[64,1792]{1,0:T(8,128)(2,1)}, bf16[64,1792]{1,0:T(8,128)(2,1)S(1)}) custom-call(s32[4]{0:T(128)S(1)} %pad_add_fusion.place_ref.refs_0_, bf16[512,512]{1,0:T(8,128)(2,1)S(1)} %get-tuple-element.52.refs_1_, ...), custom_call_target="tpu_custom_call" | custom-call | tf_op jit(solution)/shard_map/pallas_call | solution.py:52
  88.5 1.2 collective-permute-start.21
  89.7 1.7 %collective-permute-start.22 = (bf16[64,1792]{1,0:T(8,128)(2,1)}, bf16[64,1792]{1,0:T(8,128)(2,1)S(1)}, u32[]{:S(2)}, u32[]{:S(2)}) collective-permute-start(bf16[64,1792]{1,0:T(8,128)(2,1)} %get-tuple-element.58), channel_id=1, source_target_pairs={{0,32},{16,48},{32,64},{48,80},{64,96},{80,112},{96,0},{112,16},{2... | collective-permute-start | bytes 688136 | tf_op jit(solution)/shard_map/ppermute | solution.py:44
  91.5 4.2 %collective-permute-start.23 = (bf16[64,1792]{1,0:T(8,128)(2,1)}, bf16[64,1792]{1,0:T(8,128)(2,1)S(1)}, u32[]{:S(2)}, u32[]{:S(2)}) collective-permute-start(bf16[64,1792]{1,0:T(8,128)(2,1)} %get-tuple-element.59), channel_id=1, source_target_pairs={{0,112},{16,0},{32,16},{48,32},{64,48},{80,64},{96,80},{112,96},{2... | collective-permute-start | bytes 688136 | tf_op jit(solution)/shard_map/ppermute | solution.py:44
  96.8 1.3 %convolution_convert_fusion.refs_2_ = bf16[4,32,512]{2,1,0:T(8,128)(2,1)S(1)} fusion(bf16[4,256,512]{2,1,0:T(8,128)(2,1)S(1)} %copy-done, f32[4,32]{1,0:T(4,128)S(1)} %fusion.9, f32[4,32,256]{2,1,0:T(8,128)} %copy-done.5, pred[4,256]{1,0:T(4,128)(4,1)S(1)} %iota_compare_fusion.1), kind=kOutput, calls=%fused_computation.1 | convolution fusion | flops 33751424 | bytes 1312256 | tf_op jit(solution)/shard_map/bhj,bjl->bhl/dot_general | solution.py:310
  98.2 3.1 %collective-permute-done.21.refs_4_ = bf16[64,1792]{1,0:T(8,128)(2,1)S(1)} collective-permute-done((bf16[64,1792]{1,0:T(8,128)(2,1)}, bf16[64,1792]{1,0:T(8,128)(2,1)S(1)}, u32[]{:S(2)}, u32[]{:S(2)}) %collective-permute-start.21) | collective-permute-done | bytes 229408 | tf_op jit(solution)/shard_map/ppermute | solution.py:44
  101.7 1.1 collective-permute-done.23.refs_4_
  102.8 2.6 %collective-permute-done.24.refs_5_ = bf16[64,1792]{1,0:T(8,128)(2,1)S(1)} collective-permute-done((bf16[64,1792]{1,0:T(8,128)(2,1)}, bf16[64,1792]{1,0:T(8,128)(2,1)S(1)}, u32[]{:S(2)}, u32[]{:S(2)}) %collective-permute-start.24) | collective-permute-done | bytes 229408 | tf_op jit(solution)/shard_map/ppermute | solution.py:44
  105.8 14.8 %all_to_all.11.share_ref = bf16[8,16,1792]{2,1,0:T(8,128)(2,1)S(1)} all-to-all(bf16[8,16,1792]{2,1,0:T(8,128)(2,1)S(1)} %shard_map.129), channel_id=1, replica_groups={{0,2,4,6,8,10,12,14},{16,18,20,22,24,26,28,30},{32,34,36,38,40,42,44,46..., dimensions={0} | all-to-all | bytes 917504 | tf_op jit(solution)/shard_map/all_to_all | solution.py:434
  (62 shorter events, 11.1 us)
Async XLA Ops:
  39.7 16.7 %collective-permute-start.1 = (bf16[64,1792]{1,0:T(8,128)(2,1)S(1)}, bf16[64,1792]{1,0:T(8,128)(2,1)S(1)}, u32[]{:S(2)}, u32[]{:S(2)}) collective-permute-start(bf16[64,1792]{1,0:T(8,128)(2,1)S(1)} %get-tuple-element.38), channel_id=1, source_target_pairs={{0,64},{16,80},{32,96},{48,112},{64,0},{80,16},{96,32},{112,48},{2... | collective-permute-start | bytes 688136 | tf_op jit(solution)/shard_map/ppermute | solution.py:44
  39.9 16.5 %collective-permute-start.2 = (bf16[64,1792]{1,0:T(8,128)(2,1)S(1)}, bf16[64,1792]{1,0:T(8,128)(2,1)S(1)}, u32[]{:S(2)}, u32[]{:S(2)}) collective-permute-start(bf16[64,1792]{1,0:T(8,128)(2,1)S(1)} %get-tuple-element.46), channel_id=1, source_target_pairs={{0,48},{16,64},{32,80},{48,96},{64,112},{80,0},{96,16},{112,32},{2... | collective-permute-start | bytes 688136 | tf_op jit(solution)/shard_map/ppermute | solution.py:44
  40.3 19.3 %collective-permute-start.3 = (bf16[64,1792]{1,0:T(8,128)(2,1)S(1)}, bf16[64,1792]{1,0:T(8,128)(2,1)S(1)}, u32[]{:S(2)}, u32[]{:S(2)}) collective-permute-start(bf16[64,1792]{1,0:T(8,128)(2,1)S(1)} %get-tuple-element.47), channel_id=1, source_target_pairs={{0,80},{16,96},{32,112},{48,0},{64,16},{80,32},{96,48},{112,64},{2... | collective-permute-start | bytes 688136 | tf_op jit(solution)/shard_map/ppermute | solution.py:44
  45.0 14.8 %collective-permute-start.4 = (bf16[64,1792]{1,0:T(8,128)(2,1)S(1)}, bf16[64,1792]{1,0:T(8,128)(2,1)S(1)}, u32[]{:S(2)}, u32[]{:S(2)}) collective-permute-start(bf16[64,1792]{1,0:T(8,128)(2,1)S(1)} %get-tuple-element.48), channel_id=1, source_target_pairs={{0,32},{16,48},{32,64},{48,80},{64,96},{80,112},{96,0},{112,16},{2... | collective-permute-start | bytes 688136 | tf_op jit(solution)/shard_map/ppermute | solution.py:44
  45.0 15.1 %collective-permute-start.5 = (bf16[64,1792]{1,0:T(8,128)(2,1)S(1)}, bf16[64,1792]{1,0:T(8,128)(2,1)S(1)}, u32[]{:S(2)}, u32[]{:S(2)}) collective-permute-start(bf16[64,1792]{1,0:T(8,128)(2,1)S(1)} %get-tuple-element.49), channel_id=1, source_target_pairs={{0,96},{16,112},{32,0},{48,16},{64,32},{80,48},{96,64},{112,80},{2... | collective-permute-start | bytes 688136 | tf_op jit(solution)/shard_map/ppermute | solution.py:44
  56.4 7.2 %collective-permute-start.6 = (bf16[64,1792]{1,0:T(8,128)(2,1)S(1)}, bf16[64,1792]{1,0:T(8,128)(2,1)S(1)}, u32[]{:S(2)}, u32[]{:S(2)}) collective-permute-start(bf16[64,1792]{1,0:T(8,128)(2,1)S(1)} %get-tuple-element.50), channel_id=1, source_target_pairs={{0,16},{16,32},{32,48},{48,64},{64,80},{80,96},{96,112},{112,0},{2... | collective-permute-start | bytes 688136 | tf_op jit(solution)/shard_map/ppermute | solution.py:44
  56.4 7.2 %collective-permute-start.7 = (bf16[64,1792]{1,0:T(8,128)(2,1)S(1)}, bf16[64,1792]{1,0:T(8,128)(2,1)S(1)}, u32[]{:S(2)}, u32[]{:S(2)}) collective-permute-start(bf16[64,1792]{1,0:T(8,128)(2,1)S(1)} %get-tuple-element.51), channel_id=1, source_target_pairs={{0,112},{16,0},{32,16},{48,32},{64,48},{80,64},{96,80},{112,96},{2... | collective-permute-start | bytes 688136 | tf_op jit(solution)/shard_map/ppermute | solution.py:44
  59.6 4.5 %collective-permute-start.15 = (bf16[64,1792]{1,0:T(8,128)(2,1)S(1)}, bf16[64,1792]{1,0:T(8,128)(2,1)S(1)}, u32[]{:S(2)}, u32[]{:S(2)}) collective-permute-start(bf16[64,1792]{1,0:T(8,128)(2,1)S(1)} %get-tuple-element.36.refs_5_.refs_11_), channel_id=1, source_target_pairs={{0,1},{1,0},{2,3},{3,2},{4,5},{5,4},{6,7},{7,6},{8,9},{9,8},{10,11... | collective-permute-start | bytes 688136 | tf_op jit(solution)/shard_map/ppermute | solution.py:48
  59.8 4.5 %collective-permute-start.8 = (bf16[64,1792]{1,0:T(8,128)(2,1)S(1)}, bf16[64,1792]{1,0:T(8,128)(2,1)S(1)}, u32[]{:S(2)}, u32[]{:S(2)}) collective-permute-start(bf16[64,1792]{1,0:T(8,128)(2,1)S(1)} %collective-permute-done.1.refs_4_), channel_id=1, source_target_pairs={{0,1},{1,0},{2,3},{3,2},{4,5},{5,4},{6,7},{7,6},{8,9},{9,8},{10,11... | collective-permute-start | bytes 688136 | tf_op jit(solution)/shard_map/ppermute | solution.py:48
  60.2 4.5 %collective-permute-start.9 = (bf16[64,1792]{1,0:T(8,128)(2,1)S(1)}, bf16[64,1792]{1,0:T(8,128)(2,1)S(1)}, u32[]{:S(2)}, u32[]{:S(2)}) collective-permute-start(bf16[64,1792]{1,0:T(8,128)(2,1)S(1)} %collective-permute-done.2.refs_5_), channel_id=1, source_target_pairs={{0,1},{1,0},{2,3},{3,2},{4,5},{5,4},{6,7},{7,6},{8,9},{9,8},{10,11... | collective-permute-start | bytes 688136 | tf_op jit(solution)/shard_map/ppermute | solution.py:48
  63.6 1.5 %collective-permute-start.10 = (bf16[64,1792]{1,0:T(8,128)(2,1)S(1)}, bf16[64,1792]{1,0:T(8,128)(2,1)S(1)}, u32[]{:S(2)}, u32[]{:S(2)}) collective-permute-start(bf16[64,1792]{1,0:T(8,128)(2,1)S(1)} %collective-permute-done.3.refs_6_), channel_id=1, source_target_pairs={{0,1},{1,0},{2,3},{3,2},{4,5},{5,4},{6,7},{7,6},{8,9},{9,8},{10,11... | collective-permute-start | bytes 688136 | tf_op jit(solution)/shard_map/ppermute | solution.py:48
  63.6 1.8 %collective-permute-start.11 = (bf16[64,1792]{1,0:T(8,128)(2,1)S(1)}, bf16[64,1792]{1,0:T(8,128)(2,1)S(1)}, u32[]{:S(2)}, u32[]{:S(2)}) collective-permute-start(bf16[64,1792]{1,0:T(8,128)(2,1)S(1)} %collective-permute-done.4.refs_7_), channel_id=1, source_target_pairs={{0,1},{1,0},{2,3},{3,2},{4,5},{5,4},{6,7},{7,6},{8,9},{9,8},{10,11... | collective-permute-start | bytes 688136 | tf_op jit(solution)/shard_map/ppermute | solution.py:48
  64.2 1.6 %collective-permute-start.12 = (bf16[64,1792]{1,0:T(8,128)(2,1)S(1)}, bf16[64,1792]{1,0:T(8,128)(2,1)S(1)}, u32[]{:S(2)}, u32[]{:S(2)}) collective-permute-start(bf16[64,1792]{1,0:T(8,128)(2,1)S(1)} %collective-permute-done.5.refs_8_), channel_id=1, source_target_pairs={{0,1},{1,0},{2,3},{3,2},{4,5},{5,4},{6,7},{7,6},{8,9},{9,8},{10,11... | collective-permute-start | bytes 688136 | tf_op jit(solution)/shard_map/ppermute | solution.py:48
  64.3 1.8 %collective-permute-start.13 = (bf16[64,1792]{1,0:T(8,128)(2,1)S(1)}, bf16[64,1792]{1,0:T(8,128)(2,1)S(1)}, u32[]{:S(2)}, u32[]{:S(2)}) collective-permute-start(bf16[64,1792]{1,0:T(8,128)(2,1)S(1)} %collective-permute-done.6.refs_9_), channel_id=1, source_target_pairs={{0,1},{1,0},{2,3},{3,2},{4,5},{5,4},{6,7},{7,6},{8,9},{9,8},{10,11... | collective-permute-start | bytes 688136 | tf_op jit(solution)/shard_map/ppermute | solution.py:48
  64.7 1.8 %collective-permute-start.14 = (bf16[64,1792]{1,0:T(8,128)(2,1)S(1)}, bf16[64,1792]{1,0:T(8,128)(2,1)S(1)}, u32[]{:S(2)}, u32[]{:S(2)}) collective-permute-start(bf16[64,1792]{1,0:T(8,128)(2,1)S(1)} %collective-permute-done.7.refs_10_), channel_id=1, source_target_pairs={{0,1},{1,0},{2,3},{3,2},{4,5},{5,4},{6,7},{7,6},{8,9},{9,8},{10,11... | collective-permute-start | bytes 688136 | tf_op jit(solution)/shard_map/ppermute | solution.py:48
  72.8 13.5 %collective-permute-start.20 = (bf16[5,64,1792]{2,1,0:T(8,128)(2,1)S(1)}, bf16[5,64,1792]{2,1,0:T(8,128)(2,1)S(1)}, u32[]{:S(2)}, u32[]{:S(2)}) collective-permute-start(bf16[5,64,1792]{2,1,0:T(8,128)(2,1)S(1)} %shard_map.126), channel_id=1, source_target_pairs={{0,1},{1,0},{2,3},{3,2},{4,5},{5,4},{6,7},{7,6},{8,9},{9,8},{10,11... | collective-permute-start | bytes 3440648 | tf_op jit(solution)/shard_map/ppermute | solution.py:48
  73.1 3.6 %collective-permute-start.16 = (bf16[3,64,1792]{2,1,0:T(8,128)(2,1)S(1)}, bf16[3,64,1792]{2,1,0:T(8,128)(2,1)S(1)}, u32[]{:S(2)}, u32[]{:S(2)}) collective-permute-start(bf16[3,64,1792]{2,1,0:T(8,128)(2,1)S(1)} %get-tuple-element.53), channel_id=1, source_target_pairs={{0,1},{1,0},{2,3},{3,2},{4,5},{5,4},{6,7},{7,6},{8,9},{9,8},{10,11... | collective-permute-start | bytes 2064392 | tf_op jit(solution)/shard_map/ppermute | solution.py:48
  77.8 13.6 %collective-permute-start.17 = (bf16[64,1792]{1,0:T(8,128)(2,1)S(1)}, bf16[64,1792]{1,0:T(8,128)(2,1)S(1)}, u32[]{:S(2)}, u32[]{:S(2)}) collective-permute-start(bf16[64,1792]{1,0:T(8,128)(2,1)S(1)} %get-tuple-element.54), channel_id=1, source_target_pairs={{0,64},{16,80},{32,96},{48,112},{64,0},{80,16},{96,32},{112,48},{2... | collective-permute-start | bytes 688136 | tf_op jit(solution)/shard_map/ppermute | solution.py:44
  82.0 13.7 %collective-permute-start.18 = (bf16[64,1792]{1,0:T(8,128)(2,1)S(1)}, bf16[64,1792]{1,0:T(8,128)(2,1)S(1)}, u32[]{:S(2)}, u32[]{:S(2)}) collective-permute-start(bf16[64,1792]{1,0:T(8,128)(2,1)S(1)} %get-tuple-element.55), channel_id=1, source_target_pairs={{0,80},{16,96},{32,112},{48,0},{64,16},{80,32},{96,48},{112,64},{2... | collective-permute-start | bytes 688136 | tf_op jit(solution)/shard_map/ppermute | solution.py:44
  82.4 15.8 %collective-permute-start.19 = (bf16[64,1792]{1,0:T(8,128)(2,1)S(1)}, bf16[64,1792]{1,0:T(8,128)(2,1)S(1)}, u32[]{:S(2)}, u32[]{:S(2)}) collective-permute-start(bf16[64,1792]{1,0:T(8,128)(2,1)S(1)} %get-tuple-element.56), channel_id=1, source_target_pairs={{0,48},{16,64},{32,80},{48,96},{64,112},{80,0},{96,16},{112,32},{2... | collective-permute-start | bytes 688136 | tf_op jit(solution)/shard_map/ppermute | solution.py:44
  88.5 12.7 %collective-permute-start.21 = (bf16[64,1792]{1,0:T(8,128)(2,1)}, bf16[64,1792]{1,0:T(8,128)(2,1)S(1)}, u32[]{:S(2)}, u32[]{:S(2)}) collective-permute-start(bf16[64,1792]{1,0:T(8,128)(2,1)} %get-tuple-element.57), channel_id=1, source_target_pairs={{0,96},{16,112},{32,0},{48,16},{64,32},{80,48},{96,64},{112,80},{2... | collective-permute-start | bytes 688136 | tf_op jit(solution)/shard_map/ppermute | solution.py:44
  89.7 12.0 %collective-permute-start.22 = (bf16[64,1792]{1,0:T(8,128)(2,1)}, bf16[64,1792]{1,0:T(8,128)(2,1)S(1)}, u32[]{:S(2)}, u32[]{:S(2)}) collective-permute-start(bf16[64,1792]{1,0:T(8,128)(2,1)} %get-tuple-element.58), channel_id=1, source_target_pairs={{0,32},{16,48},{32,64},{48,80},{64,96},{80,112},{96,0},{112,16},{2... | collective-permute-start | bytes 688136 | tf_op jit(solution)/shard_map/ppermute | solution.py:44
  91.5 11.4 %collective-permute-start.23 = (bf16[64,1792]{1,0:T(8,128)(2,1)}, bf16[64,1792]{1,0:T(8,128)(2,1)S(1)}, u32[]{:S(2)}, u32[]{:S(2)}) collective-permute-start(bf16[64,1792]{1,0:T(8,128)(2,1)} %get-tuple-element.59), channel_id=1, source_target_pairs={{0,112},{16,0},{32,16},{48,32},{64,48},{80,64},{96,80},{112,96},{2... | collective-permute-start | bytes 688136 | tf_op jit(solution)/shard_map/ppermute | solution.py:44
  95.8 9.6 %collective-permute-start.24 = (bf16[64,1792]{1,0:T(8,128)(2,1)}, bf16[64,1792]{1,0:T(8,128)(2,1)S(1)}, u32[]{:S(2)}, u32[]{:S(2)}) collective-permute-start(bf16[64,1792]{1,0:T(8,128)(2,1)} %get-tuple-element.60), channel_id=1, source_target_pairs={{0,16},{16,32},{32,48},{48,64},{64,80},{80,96},{96,112},{112,0},{2... | collective-permute-start | bytes 688136 | tf_op jit(solution)/shard_map/ppermute | solution.py:44
  (9 other events, 134.3 us)

commit v2 on v1

--- a/solution.py
+++ b/solution.py
@@ -265,7 +265,6 @@
 
 
 def combine_kernel(place, taking_ref, sofar_ref, *refs):
-    refs = refs[1:]
     back_refs, (out_ref, rows) = refs[:-2], refs[-2:]
     slots, half = back_refs[0].shape
     depth = len(back_refs) * slots
@@ -295,22 +294,20 @@
     return high, (value - high.astype(jnp.float32)).astype(jnp.bfloat16)
 
 
-def attention(q_latent, q_rope, cache_latent, cache_rope, lengths):
-    scores = jnp.einsum("bhl,bjl->bhj", q_latent, cache_latent, preferred_element_type=jnp.float32)
-    scores = scores + jnp.einsum(
-        "bhr,brj->bhj", q_rope, cache_rope, preferred_element_type=jnp.float32
-    )
-    scores = scores * softmax_scale
-    position = jnp.arange(cache_latent.shape[1], dtype=jnp.int32)
-    live = position[None, None, :] < lengths[:, None, None]
-    scores = jnp.where(live, scores, -jnp.inf)
-    highest = jnp.max(scores, axis=2, keepdims=True)
-    expo = jnp.where(live, jnp.exp(scores - highest), 0.0)
-    attn_probs = (expo / jnp.sum(expo, axis=2, keepdims=True)).astype(jnp.bfloat16)
-    attn_latent = jnp.einsum(
-        "bhj,bjl->bhl", attn_probs, cache_latent, preferred_element_type=jnp.float32
-    )
-    return attn_latent.astype(jnp.bfloat16)
+def attention_kernel(lengths_ref, q_latent_ref, q_rope_ref, latent_ref, rope_ref, out_ref):
+    for sequence in range(q_latent_ref.shape[0]):
+        latent = latent_ref[sequence]
+        scores = lax.dot_general(
+            q_latent_ref[sequence], latent, (((1,), (1,)), ((), ())), preferred_element_type=jnp.float32
+        ) + jnp.dot(q_rope_ref[sequence], rope_ref[sequence], preferred_element_type=jnp.float32)
+        position = lax.broadcasted_iota(jnp.int32, scores.shape, 1)
+        live = position < lengths_ref[sequence]
+        scores = jnp.where(live, scores * softmax_scale, -jnp.inf)
+        highest = jnp.max(scores, axis=1, keepdims=True)
+        expo = jnp.where(live, jnp.exp(scores - highest), 0.0)
+        probs = (expo / jnp.sum(expo, axis=1, keepdims=True)).astype(jnp.bfloat16)
+        mixed = jnp.dot(probs, latent, preferred_element_type=jnp.float32)
+        out_ref[sequence] = mixed.astype(jnp.bfloat16)
 
 
 def local(
@@ -382,7 +379,11 @@
         other[step] = swapped(own[step], "tp")
     gate_w, up_w, down_w = weights
 
-    attn_latent = attention(q_latent, q_rope, cache_latent, cache_rope, lengths)
+    attn_latent = on_chip(
+        attention_kernel,
+        jax.ShapeDtypeStruct(q_latent.shape, bf16),
+        (lengths, q_latent, q_rope, cache_latent, cache_rope),
+    )
 
     all_slots = side * line_slots
     rows_scratch = pltpu.VMEM((all_slots, half), bf16)
@@ -415,8 +416,9 @@
         summed.update(zip(steps_of, parts))
 
     back = {0: summed[0]}
-    for step in order:
+    for step in order[:-1]:
         back[step] = shifted(summed[step], -step, side)
+    back[order[-1]] = shifted(summed[order[-1]], -order[-1], side)
     cut = side // 2
     half_scratch = pltpu.VMEM((cut * line_slots, half), bf16)
     sofar = on_chip(
@@ -428,7 +430,7 @@
     weighted = on_chip(
         lambda *refs: combine_kernel(cut, *refs),
         jax.ShapeDtypeStruct((side, token_count, half), bf16),
-        (taking, sofar, attn_latent, *(back[s] for s in steps[cut:])),
+        (taking, sofar, *(back[s] for s in steps[cut:])),
         (half_scratch,),
     )
     shares = lax.all_to_all(

time: 122 us -> 124 us (1.016)
  blocking collectives: 48.4 us -> 33.6 us
  waiting for transfers between devices: 18 us -> 28.7 us
  starting transfers between devices: 31.5 us -> 36 us
  Pallas kernels: 17.6 us -> 20.6 us
  matrix products: 3.03 us -> 0.96 us
    all_to_all x1 -> x0, blocking collectives: 14.8 us -> none  [local(): lax.all_to_all(weighted, pair, 0, 0, axis_index_groups=first_groups(side)...]
    all_to_all x0 -> x1, waiting for transfers between devices: none -> 7.99 us  [local(): lax.all_to_all(weighted, pair, 0, 0, axis_index_groups=first_groups(side)...]
    all_to_all x0 -> x1, starting transfers between devices: none -> 4.75 us  [local(): lax.all_to_all(weighted, pair, 0, 0, axis_index_groups=first_groups(side)...]
    pallas_call x9 -> x10, Pallas kernels: 13.3 us -> 16.4 us  [on_chip(): pl.pallas_call(kernel, out_shape=out_shapes, in_specs=[pl.BlockSpec(memor...]
    ppermute x14, waiting for transfers between devices: 13.5 us -> 15.8 us  [shifted(): return lax.ppermute(value, pair, moves)]
    dot_general x3 -> x0, matrix products: 1.83 us -> none  [the longest x1 1.28 us: attention(): jnp.einsum('bhj,bjl->bhl', attn_probs, cache_latent, preferred_element_ty...]
  transfers between devices with their start and end apart: 25 -> 26, of which waited for: 14 -> 17; matrix products, arithmetic and copies ran while one was open for 2% -> 1% of each run, Pallas kernels for 7% -> 8%
where the time goes in v2:
time: 124 us; the launch traced here: 123 us
  starting transfers between devices  36 us (29%)
  blocking collectives  33.6 us (27%)
  waiting for transfers between devices  28.7 us (23%)
  Pallas kernels  20.6 us (17%)
  local copies, waits for them, and re-layouts  1.79 us (1%)
    all_to_all x1, blocking collectives, local(): lax.all_to_all(message, pair, 0, 0, axis_index_groups=first_groups(side),...  33.6 us
    ppermute x14, starting transfers between devices, shifted(): return lax.ppermute(value, pair, moves)  28.7 us
    pallas_call x10, Pallas kernels, on_chip(): pl.pallas_call(kernel, out_shape=out_shapes, in_specs=[pl.BlockSpec(memor...  16.4 us
    ppermute x14, waiting for transfers between devices, shifted(): return lax.ppermute(value, pair, moves)  15.8 us
    all_to_all x1, waiting for transfers between devices, local(): lax.all_to_all(weighted, pair, 0, 0, axis_index_groups=first_groups(side)...  7.99 us
    ppermute x11, waiting for transfers between devices, swapped(): return lax.ppermute(value, axis, [(0, 1), (1, 0)])  4.99 us
    all_to_all x1, starting transfers between devices, local(): lax.all_to_all(weighted, pair, 0, 0, axis_index_groups=first_groups(side)...  4.75 us
    pallas_call x1, Pallas kernels, fetched(): pl.pallas_call(lambda *refs: fetch_kernel(side, *refs), out_shape=tuple((...  4.23 us
  transfers between devices with their start and end apart: 26, of which 17 were waited for; matrix products, arithmetic and copies ran while one was open for 1% of the time, Pallas kernels for 8%

profile of v2, /device:TPU:514, one launch (start us, length us, event | category | flops | bytes accessed | tf_op | source)
XLA Modules:
  0.0 123.5 jit_solution(18138289413666560006)
XLA Ops:
  5.4 33.6 %all_to_all.10.refs_1_ = bf16[8,16,1920]{2,1,0:T(8,128)(2,1)S(1)} all-to-all(bf16[8,16,1920]{2,1,0:T(8,128)(2,1)S(1)} %get-tuple-element.33), channel_id=1, replica_groups={{0,2,4,6,8,10,12,14},{16,18,20,22,24,26,28,30},{32,34,36,38,40,42,44,46..., dimensions={0} | all-to-all | bytes 983040 | tf_op jit(solution)/shard_map/all_to_all | solution.py:356
  39.0 1.4 %shard_map.123 = (bf16[64,1792]{1,0:T(8,128)(2,1)S(1)}, bf16[64,1792]{1,0:T(8,128)(2,1)S(1)}, bf16[64,1792]{1,0:T(8,128)(2,1)S(1)}, bf16[64,1792]{1,0:T(8,128)(2...) custom-call(s32[4]{0:T(128)S(1)} %pad_add_fusion.place_ref.refs_0_, ...), custom_call_target="tpu_custom_call" | custom-call | tf_op jit(solution)/shard_map/pallas_call | solution.py:52
  41.0 4.7 %collective-permute-start.3 = (bf16[64,1792]{1,0:T(8,128)(2,1)S(1)}, bf16[64,1792]{1,0:T(8,128)(2,1)S(1)}, u32[]{:S(2)}, u32[]{:S(2)}) collective-permute-start(bf16[64,1792]{1,0:T(8,128)(2,1)S(1)} %get-tuple-element.47), channel_id=1, source_target_pairs={{0,80},{16,96},{32,112},{48,0},{64,16},{80,32},{96,48},{112,64},{2... | collective-permute-start | bytes 688136 | tf_op jit(solution)/shard_map/ppermute | solution.py:44
  45.7 4.1 %collective-permute-start.5 = (bf16[64,1792]{1,0:T(8,128)(2,1)S(1)}, bf16[64,1792]{1,0:T(8,128)(2,1)S(1)}, u32[]{:S(2)}, u32[]{:S(2)}) collective-permute-start(bf16[64,1792]{1,0:T(8,128)(2,1)S(1)} %get-tuple-element.49), channel_id=1, source_target_pairs={{0,96},{16,112},{32,0},{48,16},{64,32},{80,48},{96,64},{112,80},{2... | collective-permute-start | bytes 688136 | tf_op jit(solution)/shard_map/ppermute | solution.py:44
  49.9 4.2 %fetch_weights.1 = (bf16[3584,512]{1,0:T(8,128)(2,1)S(1)}, bf16[3584,512]{1,0:T(8,128)(2,1)S(1)}, bf16[512,3584]{1,0:T(8,128)(2,1)S(1)}, bf16[256,512]{1,0:T(8,128)(2,1)S(1)}) custom-call(bf16[3584,512]{1,0:T(8,128)(2,1)} %bitcast.10, bf16[3584,512]{1,0:T(8,128)(2,1)} %bitcast.11, bf16[512,3584]{1,0:T(8,128)(2,1)} %bitcast.12, ...), custom_call_target="tpu_custom_call" | custom-call | tf_op jit(solution)/shard_map/fetch_weights/pallas_call | solution.py:124
  54.1 3.0 %collective-permute-done.1.refs_4_ = bf16[64,1792]{1,0:T(8,128)(2,1)S(1)} collective-permute-done((bf16[64,1792]{1,0:T(8,128)(2,1)S(1)}, bf16[64,1792]{1,0:T(8,128)(2,1)S(1)}, u32[]{:S(2)}, u32[]{:S(2)}) %collective-permute-start.1) | collective-permute-done | bytes 229408 | tf_op jit(solution)/shard_map/ppermute | solution.py:44
  57.1 3.2 %collective-permute-start.7 = (bf16[64,1792]{1,0:T(8,128)(2,1)S(1)}, bf16[64,1792]{1,0:T(8,128)(2,1)S(1)}, u32[]{:S(2)}, u32[]{:S(2)}) collective-permute-start(bf16[64,1792]{1,0:T(8,128)(2,1)S(1)} %get-tuple-element.51), channel_id=1, source_target_pairs={{0,112},{16,0},{32,16},{48,32},{64,48},{80,64},{96,80},{112,96},{2... | collective-permute-start | bytes 688136 | tf_op jit(solution)/shard_map/ppermute | solution.py:44
  61.0 3.3 %collective-permute-done.6.refs_9_ = bf16[64,1792]{1,0:T(8,128)(2,1)S(1)} collective-permute-done((bf16[64,1792]{1,0:T(8,128)(2,1)S(1)}, bf16[64,1792]{1,0:T(8,128)(2,1)S(1)}, u32[]{:S(2)}, u32[]{:S(2)}) %collective-permute-start.6) | collective-permute-done | bytes 229408 | tf_op jit(solution)/shard_map/ppermute | solution.py:44
  67.1 5.0 %shard_map.124 = (bf16[512,512]{1,0:T(8,128)(2,1)S(1)}, bf16[3,64,1792]{2,1,0:T(8,128)(2,1)S(1)}) custom-call(s32[4]{0:T(128)S(1)} %pad_add_fusion.place_ref.refs_0_, bf16[3584,512]{1,0:T(8,128)(2,1)S(1)} %get-tuple-element.42.refs_1_, bf16[3584,512]{1,0:T(8,128)(2,1)S(1)} %get-tuple-element.43.refs_2_, ...), custom_call_target="tpu_custom_call" | custom-call | tf_op jit(solution)/shard_map/pallas_call | solution.py:52
  72.2 1.3 %shard_map.126 = bf16[5,64,1792]{2,1,0:T(8,128)(2,1)S(1)} custom-call(s32[4]{0:T(128)S(1)} %pad_add_fusion.place_ref.refs_0_, bf16[512,512]{1,0:T(8,128)(2,1)S(1)} %get-tuple-element.52.refs_1_, bf16[512,3584]{1,0:T(8,128)(2,1)S(1)} %get-tuple-element.44.refs_3_.refs_2_), custom_call_target="tpu_custom_call" | custom-call | tf_op jit(solution)/shard_map/pallas_call | solution.py:52
  74.1 3.3 %collective-permute-done.16.refs_3_ = bf16[3,64,1792]{2,1,0:T(8,128)(2,1)S(1)} collective-permute-done((bf16[3,64,1792]{2,1,0:T(8,128)(2,1)S(1)}, bf16[3,64,1792]{2,1,0:T(8,128)(2,1)S(1)}, u32[]{:S(2)}, u32[]{:S(2)}) %collective-permute-start.16) | collective-permute-done | bytes 688160 | tf_op jit(solution)/shard_map/ppermute | solution.py:48
  78.5 4.2 %collective-permute-start.17 = (bf16[64,1792]{1,0:T(8,128)(2,1)S(1)}, bf16[64,1792]{1,0:T(8,128)(2,1)S(1)}, u32[]{:S(2)}, u32[]{:S(2)}) collective-permute-start(bf16[64,1792]{1,0:T(8,128)(2,1)S(1)} %get-tuple-element.54), channel_id=1, source_target_pairs={{0,64},{16,80},{32,96},{48,112},{64,0},{80,16},{96,32},{112,48},{2... | collective-permute-start | bytes 688136 | tf_op jit(solution)/shard_map/ppermute | solution.py:44
  82.7 3.8 %collective-permute-start.19 = (bf16[64,1792]{1,0:T(8,128)(2,1)S(1)}, bf16[64,1792]{1,0:T(8,128)(2,1)S(1)}, u32[]{:S(2)}, u32[]{:S(2)}) collective-permute-start(bf16[64,1792]{1,0:T(8,128)(2,1)S(1)} %get-tuple-element.56), channel_id=1, source_target_pairs={{0,48},{16,64},{32,80},{48,96},{64,112},{80,0},{96,16},{112,32},{2... | collective-permute-start | bytes 688136 | tf_op jit(solution)/shard_map/ppermute | solution.py:44
  86.5 1.3 %shard_map.127 = (bf16[64,1792]{1,0:T(8,128)(2,1)S(1)}, bf16[64,1792]{1,0:T(8,128)(2,1)S(1)}, bf16[64,1792]{1,0:T(8,128)(2,1)S(1)}, bf16[64,1792]{1,0:T(8,128)(2,1)S(1)}, bf16[64,1792]{1,0:T(8,128)(2,1)S(1)}) custom-call(s32[4]{0:T(128)S(1)} %pad_add_fusion.place_ref.refs_0_, bf16[512,512]{1,0:T(8,128)(2,1)S(1)} %get-tuple-element.52.refs_1_, ...), custom_call_target="tpu_custom_call" | custom-call | tf_op jit(solution)/shard_map/pallas_call | solution.py:52
  87.9 1.3 %collective-permute-start.21 = (bf16[64,1792]{1,0:T(8,128)(2,1)S(1)}, bf16[64,1792]{1,0:T(8,128)(2,1)S(1)}, u32[]{:S(2)}, u32[]{:S(2)}) collective-permute-start(bf16[64,1792]{1,0:T(8,128)(2,1)S(1)} %get-tuple-element.57), channel_id=1, source_target_pairs={{0,96},{16,112},{32,0},{48,16},{64,32},{80,48},{96,64},{112,80},{2... | collective-permute-start | bytes 688136 | tf_op jit(solution)/shard_map/ppermute | solution.py:44
  89.2 1.7 %collective-permute-start.22 = (bf16[64,1792]{1,0:T(8,128)(2,1)S(1)}, bf16[64,1792]{1,0:T(8,128)(2,1)S(1)}, u32[]{:S(2)}, u32[]{:S(2)}) collective-permute-start(bf16[64,1792]{1,0:T(8,128)(2,1)S(1)} %get-tuple-element.58), channel_id=1, source_target_pairs={{0,32},{16,48},{32,64},{48,80},{64,96},{80,112},{96,0},{112,16},{2... | collective-permute-start | bytes 688136 | tf_op jit(solution)/shard_map/ppermute | solution.py:44
  91.2 3.9 %collective-permute-start.23 = (bf16[64,1792]{1,0:T(8,128)(2,1)S(1)}, bf16[64,1792]{1,0:T(8,128)(2,1)S(1)}, u32[]{:S(2)}, u32[]{:S(2)}) collective-permute-start(bf16[64,1792]{1,0:T(8,128)(2,1)S(1)} %get-tuple-element.59), channel_id=1, source_target_pairs={{0,112},{16,0},{32,16},{48,32},{64,48},{80,64},{96,80},{112,96},{2... | collective-permute-start | bytes 688136 | tf_op jit(solution)/shard_map/ppermute | solution.py:44
  95.1 1.3 %collective-permute-done.18.refs_2_ = bf16[64,1792]{1,0:T(8,128)(2,1)S(1)} collective-permute-done((bf16[64,1792]{1,0:T(8,128)(2,1)S(1)}, bf16[64,1792]{1,0:T(8,128)(2,1)S(1)}, u32[]{:S(2)}, u32[]{:S(2)}) %collective-permute-start.18) | collective-permute-done | bytes 229408 | tf_op jit(solution)/shard_map/ppermute | solution.py:44
  98.6 3.3 %collective-permute-done.21.refs_4_ = bf16[64,1792]{1,0:T(8,128)(2,1)S(1)} collective-permute-done((bf16[64,1792]{1,0:T(8,128)(2,1)S(1)}, bf16[64,1792]{1,0:T(8,128)(2,1)S(1)}, u32[]{:S(2)}, u32[]{:S(2)}) %collective-permute-start.21) | collective-permute-done | bytes 229408 | tf_op jit(solution)/shard_map/ppermute | solution.py:44
  103.4 2.2 %collective-permute-done.24.refs_4_ = bf16[64,1792]{1,0:T(8,128)(2,1)S(1)} collective-permute-done((bf16[64,1792]{1,0:T(8,128)(2,1)S(1)}, bf16[64,1792]{1,0:T(8,128)(2,1)S(1)}, u32[]{:S(2)}, u32[]{:S(2)}) %collective-permute-start.24) | collective-permute-done | bytes 229408 | tf_op jit(solution)/shard_map/ppermute | solution.py:44
  105.6 1.2 shard_map.129
  106.8 4.8 %all-to-all-start.1 = ((bf16[8,16,1792]{2,1,0:T(8,128)(2,1)}), bf16[8,16,1792]{2,1,0:T(8,128)(2,1)S(1)}, u32[]{:S(2)}, u32[]{:S(2)}) async-start(bf16[8,16,1792]{2,1,0:T(8,128)(2,1)} %shard_map.129), calls=%async_computation.1 | async-start | bytes 917504 | tf_op jit(solution)/shard_map/all_to_all | solution.py:436
  111.6 3.2 %shard_map.131 = bf16[4,32,512]{2,1,0:T(8,128)(2,1)} custom-call(s32[4]{0:T(128)S(1)} %copy-done.6, bf16[4,32,512]{2,1,0:T(8,128)(2,1)S(1)} %copy-done.3, bf16[4,32,64]{2,1,0:T(8,128)(2,1)S(1)} %copy-done.5, bf16[4,256,512]{2,1,0:T(8,128)(2,1)S(1)} %copy-done.1, bf16[4,64,256]{2,1,0:T(8,128)(2,1)S(1)} %copy-done.4), custom_call_target="tpu_custom_call" | custom-call | tf_op jit(solution)/shard_map/pallas_call | solution.py:52
  114.8 8.0 %all-to-all-done.1.share_ref = bf16[8,16,1792]{2,1,0:T(8,128)(2,1)S(1)} async-done(((bf16[8,16,1792]{2,1,0:T(8,128)(2,1)}), bf16[8,16,1792]{2,1,0:T(8,128)(2,1)S(1)}, u32[]{:S(2)}, u32[]{:S(2)}) %all-to-all-start.1) | async-done | bytes 458784 | tf_op jit(solution)/shard_map/all_to_all | solution.py:436
  (57 shorter events, 15.3 us)
Async XLA Ops:
  40.4 16.7 %collective-permute-start.1 = (bf16[64,1792]{1,0:T(8,128)(2,1)S(1)}, bf16[64,1792]{1,0:T(8,128)(2,1)S(1)}, u32[]{:S(2)}, u32[]{:S(2)}) collective-permute-start(bf16[64,1792]{1,0:T(8,128)(2,1)S(1)} %get-tuple-element.38), channel_id=1, source_target_pairs={{0,64},{16,80},{32,96},{48,112},{64,0},{80,16},{96,32},{112,48},{2... | collective-permute-start | bytes 688136 | tf_op jit(solution)/shard_map/ppermute | solution.py:44
  40.6 16.5 %collective-permute-start.2 = (bf16[64,1792]{1,0:T(8,128)(2,1)S(1)}, bf16[64,1792]{1,0:T(8,128)(2,1)S(1)}, u32[]{:S(2)}, u32[]{:S(2)}) collective-permute-start(bf16[64,1792]{1,0:T(8,128)(2,1)S(1)} %get-tuple-element.46), channel_id=1, source_target_pairs={{0,48},{16,64},{32,80},{48,96},{64,112},{80,0},{96,16},{112,32},{2... | collective-permute-start | bytes 688136 | tf_op jit(solution)/shard_map/ppermute | solution.py:44
  41.0 19.3 %collective-permute-start.3 = (bf16[64,1792]{1,0:T(8,128)(2,1)S(1)}, bf16[64,1792]{1,0:T(8,128)(2,1)S(1)}, u32[]{:S(2)}, u32[]{:S(2)}) collective-permute-start(bf16[64,1792]{1,0:T(8,128)(2,1)S(1)} %get-tuple-element.47), channel_id=1, source_target_pairs={{0,80},{16,96},{32,112},{48,0},{64,16},{80,32},{96,48},{112,64},{2... | collective-permute-start | bytes 688136 | tf_op jit(solution)/shard_map/ppermute | solution.py:44
  45.7 14.8 %collective-permute-start.4 = (bf16[64,1792]{1,0:T(8,128)(2,1)S(1)}, bf16[64,1792]{1,0:T(8,128)(2,1)S(1)}, u32[]{:S(2)}, u32[]{:S(2)}) collective-permute-start(bf16[64,1792]{1,0:T(8,128)(2,1)S(1)} %get-tuple-element.48), channel_id=1, source_target_pairs={{0,32},{16,48},{32,64},{48,80},{64,96},{80,112},{96,0},{112,16},{2... | collective-permute-start | bytes 688136 | tf_op jit(solution)/shard_map/ppermute | solution.py:44
  45.7 15.1 %collective-permute-start.5 = (bf16[64,1792]{1,0:T(8,128)(2,1)S(1)}, bf16[64,1792]{1,0:T(8,128)(2,1)S(1)}, u32[]{:S(2)}, u32[]{:S(2)}) collective-permute-start(bf16[64,1792]{1,0:T(8,128)(2,1)S(1)} %get-tuple-element.49), channel_id=1, source_target_pairs={{0,96},{16,112},{32,0},{48,16},{64,32},{80,48},{96,64},{112,80},{2... | collective-permute-start | bytes 688136 | tf_op jit(solution)/shard_map/ppermute | solution.py:44
  57.1 7.2 %collective-permute-start.6 = (bf16[64,1792]{1,0:T(8,128)(2,1)S(1)}, bf16[64,1792]{1,0:T(8,128)(2,1)S(1)}, u32[]{:S(2)}, u32[]{:S(2)}) collective-permute-start(bf16[64,1792]{1,0:T(8,128)(2,1)S(1)} %get-tuple-element.50), channel_id=1, source_target_pairs={{0,16},{16,32},{32,48},{48,64},{64,80},{80,96},{96,112},{112,0},{2... | collective-permute-start | bytes 688136 | tf_op jit(solution)/shard_map/ppermute | solution.py:44
  57.1 7.2 %collective-permute-start.7 = (bf16[64,1792]{1,0:T(8,128)(2,1)S(1)}, bf16[64,1792]{1,0:T(8,128)(2,1)S(1)}, u32[]{:S(2)}, u32[]{:S(2)}) collective-permute-start(bf16[64,1792]{1,0:T(8,128)(2,1)S(1)} %get-tuple-element.51), channel_id=1, source_target_pairs={{0,112},{16,0},{32,16},{48,32},{64,48},{80,64},{96,80},{112,96},{2... | collective-permute-start | bytes 688136 | tf_op jit(solution)/shard_map/ppermute | solution.py:44
  60.3 4.5 %collective-permute-start.15 = (bf16[64,1792]{1,0:T(8,128)(2,1)S(1)}, bf16[64,1792]{1,0:T(8,128)(2,1)S(1)}, u32[]{:S(2)}, u32[]{:S(2)}) collective-permute-start(bf16[64,1792]{1,0:T(8,128)(2,1)S(1)} %get-tuple-element.36.refs_5_.refs_11_), channel_id=1, source_target_pairs={{0,1},{1,0},{2,3},{3,2},{4,5},{5,4},{6,7},{7,6},{8,9},{9,8},{10,11... | collective-permute-start | bytes 688136 | tf_op jit(solution)/shard_map/ppermute | solution.py:48
  60.5 4.5 %collective-permute-start.8 = (bf16[64,1792]{1,0:T(8,128)(2,1)S(1)}, bf16[64,1792]{1,0:T(8,128)(2,1)S(1)}, u32[]{:S(2)}, u32[]{:S(2)}) collective-permute-start(bf16[64,1792]{1,0:T(8,128)(2,1)S(1)} %collective-permute-done.1.refs_4_), channel_id=1, source_target_pairs={{0,1},{1,0},{2,3},{3,2},{4,5},{5,4},{6,7},{7,6},{8,9},{9,8},{10,11... | collective-permute-start | bytes 688136 | tf_op jit(solution)/shard_map/ppermute | solution.py:48
  60.9 4.5 %collective-permute-start.9 = (bf16[64,1792]{1,0:T(8,128)(2,1)S(1)}, bf16[64,1792]{1,0:T(8,128)(2,1)S(1)}, u32[]{:S(2)}, u32[]{:S(2)}) collective-permute-start(bf16[64,1792]{1,0:T(8,128)(2,1)S(1)} %collective-permute-done.2.refs_5_), channel_id=1, source_target_pairs={{0,1},{1,0},{2,3},{3,2},{4,5},{5,4},{6,7},{7,6},{8,9},{9,8},{10,11... | collective-permute-start | bytes 688136 | tf_op jit(solution)/shard_map/ppermute | solution.py:48
  64.3 1.8 %collective-permute-start.11 = (bf16[64,1792]{1,0:T(8,128)(2,1)S(1)}, bf16[64,1792]{1,0:T(8,128)(2,1)S(1)}, u32[]{:S(2)}, u32[]{:S(2)}) collective-permute-start(bf16[64,1792]{1,0:T(8,128)(2,1)S(1)} %collective-permute-done.4.refs_7_), channel_id=1, source_target_pairs={{0,1},{1,0},{2,3},{3,2},{4,5},{5,4},{6,7},{7,6},{8,9},{9,8},{10,11... | collective-permute-start | bytes 688136 | tf_op jit(solution)/shard_map/ppermute | solution.py:48
  64.8 1.6 %collective-permute-start.12 = (bf16[64,1792]{1,0:T(8,128)(2,1)S(1)}, bf16[64,1792]{1,0:T(8,128)(2,1)S(1)}, u32[]{:S(2)}, u32[]{:S(2)}) collective-permute-start(bf16[64,1792]{1,0:T(8,128)(2,1)S(1)} %collective-permute-done.5.refs_8_), channel_id=1, source_target_pairs={{0,1},{1,0},{2,3},{3,2},{4,5},{5,4},{6,7},{7,6},{8,9},{9,8},{10,11... | collective-permute-start | bytes 688136 | tf_op jit(solution)/shard_map/ppermute | solution.py:48
  65.0 1.8 %collective-permute-start.13 = (bf16[64,1792]{1,0:T(8,128)(2,1)S(1)}, bf16[64,1792]{1,0:T(8,128)(2,1)S(1)}, u32[]{:S(2)}, u32[]{:S(2)}) collective-permute-start(bf16[64,1792]{1,0:T(8,128)(2,1)S(1)} %collective-permute-done.6.refs_9_), channel_id=1, source_target_pairs={{0,1},{1,0},{2,3},{3,2},{4,5},{5,4},{6,7},{7,6},{8,9},{9,8},{10,11... | collective-permute-start | bytes 688136 | tf_op jit(solution)/shard_map/ppermute | solution.py:48
  65.4 1.8 %collective-permute-start.14 = (bf16[64,1792]{1,0:T(8,128)(2,1)S(1)}, bf16[64,1792]{1,0:T(8,128)(2,1)S(1)}, u32[]{:S(2)}, u32[]{:S(2)}) collective-permute-start(bf16[64,1792]{1,0:T(8,128)(2,1)S(1)} %collective-permute-done.7.refs_10_), channel_id=1, source_target_pairs={{0,1},{1,0},{2,3},{3,2},{4,5},{5,4},{6,7},{7,6},{8,9},{9,8},{10,11... | collective-permute-start | bytes 688136 | tf_op jit(solution)/shard_map/ppermute | solution.py:48
  73.5 13.0 %collective-permute-start.20 = (bf16[5,64,1792]{2,1,0:T(8,128)(2,1)S(1)}, bf16[5,64,1792]{2,1,0:T(8,128)(2,1)S(1)}, u32[]{:S(2)}, u32[]{:S(2)}) collective-permute-start(bf16[5,64,1792]{2,1,0:T(8,128)(2,1)S(1)} %shard_map.126), channel_id=1, source_target_pairs={{0,1},{1,0},{2,3},{3,2},{4,5},{5,4},{6,7},{7,6},{8,9},{9,8},{10,11... | collective-permute-start | bytes 3440648 | tf_op jit(solution)/shard_map/ppermute | solution.py:48
  73.8 3.6 %collective-permute-start.16 = (bf16[3,64,1792]{2,1,0:T(8,128)(2,1)S(1)}, bf16[3,64,1792]{2,1,0:T(8,128)(2,1)S(1)}, u32[]{:S(2)}, u32[]{:S(2)}) collective-permute-start(bf16[3,64,1792]{2,1,0:T(8,128)(2,1)S(1)} %get-tuple-element.53), channel_id=1, source_target_pairs={{0,1},{1,0},{2,3},{3,2},{4,5},{5,4},{6,7},{7,6},{8,9},{9,8},{10,11... | collective-permute-start | bytes 2064392 | tf_op jit(solution)/shard_map/ppermute | solution.py:48
  78.5 12.7 %collective-permute-start.17 = (bf16[64,1792]{1,0:T(8,128)(2,1)S(1)}, bf16[64,1792]{1,0:T(8,128)(2,1)S(1)}, u32[]{:S(2)}, u32[]{:S(2)}) collective-permute-start(bf16[64,1792]{1,0:T(8,128)(2,1)S(1)} %get-tuple-element.54), channel_id=1, source_target_pairs={{0,64},{16,80},{32,96},{48,112},{64,0},{80,16},{96,32},{112,48},{2... | collective-permute-start | bytes 688136 | tf_op jit(solution)/shard_map/ppermute | solution.py:44
  82.7 13.7 %collective-permute-start.18 = (bf16[64,1792]{1,0:T(8,128)(2,1)S(1)}, bf16[64,1792]{1,0:T(8,128)(2,1)S(1)}, u32[]{:S(2)}, u32[]{:S(2)}) collective-permute-start(bf16[64,1792]{1,0:T(8,128)(2,1)S(1)} %get-tuple-element.55), channel_id=1, source_target_pairs={{0,80},{16,96},{32,112},{48,0},{64,16},{80,32},{96,48},{112,64},{2... | collective-permute-start | bytes 688136 | tf_op jit(solution)/shard_map/ppermute | solution.py:44
  82.7 15.9 %collective-permute-start.19 = (bf16[64,1792]{1,0:T(8,128)(2,1)S(1)}, bf16[64,1792]{1,0:T(8,128)(2,1)S(1)}, u32[]{:S(2)}, u32[]{:S(2)}) collective-permute-start(bf16[64,1792]{1,0:T(8,128)(2,1)S(1)} %get-tuple-element.56), channel_id=1, source_target_pairs={{0,48},{16,64},{32,80},{48,96},{64,112},{80,0},{96,16},{112,32},{2... | collective-permute-start | bytes 688136 | tf_op jit(solution)/shard_map/ppermute | solution.py:44
  87.9 14.0 %collective-permute-start.21 = (bf16[64,1792]{1,0:T(8,128)(2,1)S(1)}, bf16[64,1792]{1,0:T(8,128)(2,1)S(1)}, u32[]{:S(2)}, u32[]{:S(2)}) collective-permute-start(bf16[64,1792]{1,0:T(8,128)(2,1)S(1)} %get-tuple-element.57), channel_id=1, source_target_pairs={{0,96},{16,112},{32,0},{48,16},{64,32},{80,48},{96,64},{112,80},{2... | collective-permute-start | bytes 688136 | tf_op jit(solution)/shard_map/ppermute | solution.py:44
  89.2 13.1 %collective-permute-start.22 = (bf16[64,1792]{1,0:T(8,128)(2,1)S(1)}, bf16[64,1792]{1,0:T(8,128)(2,1)S(1)}, u32[]{:S(2)}, u32[]{:S(2)}) collective-permute-start(bf16[64,1792]{1,0:T(8,128)(2,1)S(1)} %get-tuple-element.58), channel_id=1, source_target_pairs={{0,32},{16,48},{32,64},{48,80},{64,96},{80,112},{96,0},{112,16},{2... | collective-permute-start | bytes 688136 | tf_op jit(solution)/shard_map/ppermute | solution.py:44
  91.2 12.2 %collective-permute-start.23 = (bf16[64,1792]{1,0:T(8,128)(2,1)S(1)}, bf16[64,1792]{1,0:T(8,128)(2,1)S(1)}, u32[]{:S(2)}, u32[]{:S(2)}) collective-permute-start(bf16[64,1792]{1,0:T(8,128)(2,1)S(1)} %get-tuple-element.59), channel_id=1, source_target_pairs={{0,112},{16,0},{32,16},{48,32},{64,48},{80,64},{96,80},{112,96},{2... | collective-permute-start | bytes 688136 | tf_op jit(solution)/shard_map/ppermute | solution.py:44
  96.4 9.2 %collective-permute-start.24 = (bf16[64,1792]{1,0:T(8,128)(2,1)S(1)}, bf16[64,1792]{1,0:T(8,128)(2,1)S(1)}, u32[]{:S(2)}, u32[]{:S(2)}) collective-permute-start(bf16[64,1792]{1,0:T(8,128)(2,1)S(1)} %get-tuple-element.60), channel_id=1, source_target_pairs={{0,16},{16,32},{32,48},{48,64},{64,80},{80,96},{96,112},{112,0},{2... | collective-permute-start | bytes 688136 | tf_op jit(solution)/shard_map/ppermute | solution.py:44
  106.8 16.0 %all-to-all-start.1 = ((bf16[8,16,1792]{2,1,0:T(8,128)(2,1)}), bf16[8,16,1792]{2,1,0:T(8,128)(2,1)S(1)}, u32[]{:S(2)}, u32[]{:S(2)}) async-start(bf16[8,16,1792]{2,1,0:T(8,128)(2,1)} %shard_map.129), calls=%async_computation.1 | async-start | bytes 917504 | tf_op jit(solution)/shard_map/all_to_all | solution.py:436
  (9 other events, 123.1 us)

commit v3 on v2

--- a/solution.py
+++ b/solution.py
@@ -59,6 +59,39 @@
         scratch_shapes=list(scratch),
         compiler_params=pltpu.CompilerParams(vmem_limit_bytes=limit * 1024 * 1024),
     )(*operands)
+
+
+def router_kernel(hidden_ref, weight_ref, logits_ref, tokens_ref, weight, sems):
+    copies = [
+        pltpu.make_async_copy(hidden_ref, tokens_ref, sems.at[0]),
+        pltpu.make_async_copy(weight_ref, weight, sems.at[1]),
+    ]
+    for copy in copies:
+        copy.start()
+    for copy in copies:
+        copy.wait()
+    logits_ref[...] = lax.dot_general(
+        tokens_ref[...], weight[...], (((1,), (1,)), ((), ())), preferred_element_type=jnp.float32
+    )
+
+
+def routed(hidden, weight):
+    vmem = pl.BlockSpec(memory_space=pltpu.VMEM)
+    return pl.pallas_call(
+        router_kernel,
+        out_shape=(
+            pltpu.VMEM((hidden.shape[0], weight.shape[0]), jnp.float32),
+            pltpu.VMEM(hidden.shape, hidden.dtype),
+        ),
+        in_specs=[pl.BlockSpec(memory_space=pltpu.HBM)] * 2,
+        out_specs=(vmem, vmem),
+        scratch_shapes=[
+            pltpu.VMEM(weight.shape, weight.dtype),
+            pltpu.SemaphoreType.DMA((2,)),
+        ],
+        compiler_params=pltpu.CompilerParams(vmem_limit_bytes=63 * 1024 * 1024 + 512 * 1024),
+        name="router",
+    )(hidden, weight)
 
 
 def message_kernel(place_ref, hidden_ref, own_ref, other_ref, mask_ref, message_ref, sum_ref):
@@ -341,7 +374,7 @@
 
     expert_iota = jnp.arange(expert_count, dtype=jnp.int32)
     mask = jnp.sum((routes.T[:, :, None] == expert_iota).astype(f32), axis=0)
-    partial_logits = jnp.dot(hidden, router_weight, preferred_element_type=f32)
+    partial_logits, hidden = routed(hidden, router_weight.T)
     other_logits = swapped(partial_logits, "tp")
 
     lanes = 128 * ((2 * side + 127) // 128)

time: 124 us -> 122 us (0.984)
  local copies, waits for them, and re-layouts: 1.79 us -> 0.03 us
    unnamed x14 -> x10, local copies, waits for them, and re-layouts: 1.79 us -> 0.03 us
where the time goes in v3:
time: 122 us
  starting transfers between devices  35.9 us (29%)
  blocking collectives  33.6 us (28%)
  waiting for transfers between devices  28.9 us (24%)
  Pallas kernels  21.8 us (18%)
    all_to_all x1, blocking collectives, local(): lax.all_to_all(message, pair, 0, 0, axis_index_groups=first_groups(side),...  33.6 us
    ppermute x14, starting transfers between devices, shifted(): return lax.ppermute(value, pair, moves)  28.6 us
    pallas_call x10, Pallas kernels, on_chip(): pl.pallas_call(kernel, out_shape=out_shapes, in_specs=[pl.BlockSpec(memor...  16.4 us
    ppermute x14, waiting for transfers between devices, shifted(): return lax.ppermute(value, pair, moves)  15.9 us
    all_to_all x1, waiting for transfers between devices, local(): lax.all_to_all(weighted, pair, 0, 0, axis_index_groups=first_groups(side)...  7.98 us
    ppermute x11, waiting for transfers between devices, swapped(): return lax.ppermute(value, axis, [(0, 1), (1, 0)])  4.99 us
    all_to_all x1, starting transfers between devices, local(): lax.all_to_all(weighted, pair, 0, 0, axis_index_groups=first_groups(side)...  4.73 us
    pallas_call x1, Pallas kernels, fetched(): pl.pallas_call(lambda *refs: fetch_kernel(side, *refs), out_shape=tuple((...  4.23 us
  transfers between devices with their start and end apart: 26, of which 17 were waited for; matrix products, arithmetic and copies ran while one was open for 1% of the time, Pallas kernels for 8%

profile of v3, /device:TPU:514, one launch (start us, length us, event | category | flops | bytes accessed | tf_op | source)
XLA Modules:
  0.0 122.0 jit_solution(3128668315529775321)
XLA Ops:
  3.9 33.6 %all_to_all.10.refs_1_ = bf16[8,16,1920]{2,1,0:T(8,128)(2,1)S(1)} all-to-all(bf16[8,16,1920]{2,1,0:T(8,128)(2,1)S(1)} %get-tuple-element.37), channel_id=1, replica_groups={{0,2,4,6,8,10,12,14},{16,18,20,22,24,26,28,30},{32,34,36,38,40,42,44,46..., dimensions={0} | all-to-all | bytes 983040 | tf_op jit(solution)/shard_map/all_to_all | solution.py:389
  37.6 1.4 %shard_map.123 = (bf16[64,1792]{1,0:T(8,128)(2,1)S(1)}, bf16[64,1792]{1,0:T(8,128)(2,1)S(1)}, bf16[64,1792]{1,0:T(8,128)(2,1)S(1)}, bf16[64,1792]{1,0:T(8,128)(2...) custom-call(s32[4]{0:T(128)S(1)} %pad_add_fusion.place_ref.refs_0_, ...), custom_call_target="tpu_custom_call" | custom-call | tf_op jit(solution)/shard_map/pallas_call | solution.py:52
  39.6 4.7 %collective-permute-start.3 = (bf16[64,1792]{1,0:T(8,128)(2,1)S(1)}, bf16[64,1792]{1,0:T(8,128)(2,1)S(1)}, u32[]{:S(2)}, u32[]{:S(2)}) collective-permute-start(bf16[64,1792]{1,0:T(8,128)(2,1)S(1)} %get-tuple-element.51), channel_id=1, source_target_pairs={{0,80},{16,96},{32,112},{48,0},{64,16},{80,32},{96,48},{112,64},{2... | collective-permute-start | bytes 688136 | tf_op jit(solution)/shard_map/ppermute | solution.py:44
  44.3 4.1 %collective-permute-start.5 = (bf16[64,1792]{1,0:T(8,128)(2,1)S(1)}, bf16[64,1792]{1,0:T(8,128)(2,1)S(1)}, u32[]{:S(2)}, u32[]{:S(2)}) collective-permute-start(bf16[64,1792]{1,0:T(8,128)(2,1)S(1)} %get-tuple-element.53), channel_id=1, source_target_pairs={{0,96},{16,112},{32,0},{48,16},{64,32},{80,48},{96,64},{112,80},{2... | collective-permute-start | bytes 688136 | tf_op jit(solution)/shard_map/ppermute | solution.py:44
  48.4 4.2 %fetch_weights.1 = (bf16[3584,512]{1,0:T(8,128)(2,1)S(1)}, bf16[3584,512]{1,0:T(8,128)(2,1)S(1)}, bf16[512,3584]{1,0:T(8,128)(2,1)S(1)}, bf16[256,512]{1,0:T(8,128)(2,1)S(1)}) custom-call(bf16[3584,512]{1,0:T(8,128)(2,1)} %bitcast.9, bf16[3584,512]{1,0:T(8,128)(2,1)} %bitcast.10, bf16[512,3584]{1,0:T(8,128)(2,1)} %bitcast.11, ...), custom_call_target="tpu_custom_call" | custom-call | tf_op jit(solution)/shard_map/fetch_weights/pallas_call | solution.py:157
  52.6 3.0 %collective-permute-done.1.refs_4_ = bf16[64,1792]{1,0:T(8,128)(2,1)S(1)} collective-permute-done((bf16[64,1792]{1,0:T(8,128)(2,1)S(1)}, bf16[64,1792]{1,0:T(8,128)(2,1)S(1)}, u32[]{:S(2)}, u32[]{:S(2)}) %collective-permute-start.1) | collective-permute-done | bytes 229408 | tf_op jit(solution)/shard_map/ppermute | solution.py:44
  55.6 3.2 %collective-permute-start.7 = (bf16[64,1792]{1,0:T(8,128)(2,1)S(1)}, bf16[64,1792]{1,0:T(8,128)(2,1)S(1)}, u32[]{:S(2)}, u32[]{:S(2)}) collective-permute-start(bf16[64,1792]{1,0:T(8,128)(2,1)S(1)} %get-tuple-element.55), channel_id=1, source_target_pairs={{0,112},{16,0},{32,16},{48,32},{64,48},{80,64},{96,80},{112,96},{2... | collective-permute-start | bytes 688136 | tf_op jit(solution)/shard_map/ppermute | solution.py:44
  59.6 3.3 %collective-permute-done.6.refs_9_ = bf16[64,1792]{1,0:T(8,128)(2,1)S(1)} collective-permute-done((bf16[64,1792]{1,0:T(8,128)(2,1)S(1)}, bf16[64,1792]{1,0:T(8,128)(2,1)S(1)}, u32[]{:S(2)}, u32[]{:S(2)}) %collective-permute-start.6) | collective-permute-done | bytes 229408 | tf_op jit(solution)/shard_map/ppermute | solution.py:44
  65.7 5.0 %shard_map.124 = (bf16[512,512]{1,0:T(8,128)(2,1)S(1)}, bf16[3,64,1792]{2,1,0:T(8,128)(2,1)S(1)}) custom-call(s32[4]{0:T(128)S(1)} %pad_add_fusion.place_ref.refs_0_, bf16[3584,512]{1,0:T(8,128)(2,1)S(1)} %get-tuple-element.46.refs_1_, bf16[3584,512]{1,0:T(8,128)(2,1)S(1)} %get-tuple-element.47.refs_2_, ...), custom_call_target="tpu_custom_call" | custom-call | tf_op jit(solution)/shard_map/pallas_call | solution.py:52
  70.7 1.3 %shard_map.126 = bf16[5,64,1792]{2,1,0:T(8,128)(2,1)S(1)} custom-call(s32[4]{0:T(128)S(1)} %pad_add_fusion.place_ref.refs_0_, bf16[512,512]{1,0:T(8,128)(2,1)S(1)} %get-tuple-element.56.refs_1_, bf16[512,3584]{1,0:T(8,128)(2,1)S(1)} %get-tuple-element.48.refs_3_.refs_2_), custom_call_target="tpu_custom_call" | custom-call | tf_op jit(solution)/shard_map/pallas_call | solution.py:52
  72.6 3.3 %collective-permute-done.16.refs_3_ = bf16[3,64,1792]{2,1,0:T(8,128)(2,1)S(1)} collective-permute-done((bf16[3,64,1792]{2,1,0:T(8,128)(2,1)S(1)}, bf16[3,64,1792]{2,1,0:T(8,128)(2,1)S(1)}, u32[]{:S(2)}, u32[]{:S(2)}) %collective-permute-start.16) | collective-permute-done | bytes 688160 | tf_op jit(solution)/shard_map/ppermute | solution.py:48
  77.0 4.2 %collective-permute-start.17 = (bf16[64,1792]{1,0:T(8,128)(2,1)S(1)}, bf16[64,1792]{1,0:T(8,128)(2,1)S(1)}, u32[]{:S(2)}, u32[]{:S(2)}) collective-permute-start(bf16[64,1792]{1,0:T(8,128)(2,1)S(1)} %get-tuple-element.58), channel_id=1, source_target_pairs={{0,64},{16,80},{32,96},{48,112},{64,0},{80,16},{96,32},{112,48},{2... | collective-permute-start | bytes 688136 | tf_op jit(solution)/shard_map/ppermute | solution.py:44
  81.2 3.8 %collective-permute-start.19 = (bf16[64,1792]{1,0:T(8,128)(2,1)S(1)}, bf16[64,1792]{1,0:T(8,128)(2,1)S(1)}, u32[]{:S(2)}, u32[]{:S(2)}) collective-permute-start(bf16[64,1792]{1,0:T(8,128)(2,1)S(1)} %get-tuple-element.60), channel_id=1, source_target_pairs={{0,48},{16,64},{32,80},{48,96},{64,112},{80,0},{96,16},{112,32},{2... | collective-permute-start | bytes 688136 | tf_op jit(solution)/shard_map/ppermute | solution.py:44
  85.0 1.3 %shard_map.127 = (bf16[64,1792]{1,0:T(8,128)(2,1)S(1)}, bf16[64,1792]{1,0:T(8,128)(2,1)S(1)}, bf16[64,1792]{1,0:T(8,128)(2,1)S(1)}, bf16[64,1792]{1,0:T(8,128)(2,1)S(1)}, bf16[64,1792]{1,0:T(8,128)(2,1)S(1)}) custom-call(s32[4]{0:T(128)S(1)} %pad_add_fusion.place_ref.refs_0_, bf16[512,512]{1,0:T(8,128)(2,1)S(1)} %get-tuple-element.56.refs_1_, ...), custom_call_target="tpu_custom_call" | custom-call | tf_op jit(solution)/shard_map/pallas_call | solution.py:52
  86.4 1.3 %collective-permute-start.21 = (bf16[64,1792]{1,0:T(8,128)(2,1)S(1)}, bf16[64,1792]{1,0:T(8,128)(2,1)S(1)}, u32[]{:S(2)}, u32[]{:S(2)}) collective-permute-start(bf16[64,1792]{1,0:T(8,128)(2,1)S(1)} %get-tuple-element.61), channel_id=1, source_target_pairs={{0,96},{16,112},{32,0},{48,16},{64,32},{80,48},{96,64},{112,80},{2... | collective-permute-start | bytes 688136 | tf_op jit(solution)/shard_map/ppermute | solution.py:44
  87.7 1.7 %collective-permute-start.22 = (bf16[64,1792]{1,0:T(8,128)(2,1)S(1)}, bf16[64,1792]{1,0:T(8,128)(2,1)S(1)}, u32[]{:S(2)}, u32[]{:S(2)}) collective-permute-start(bf16[64,1792]{1,0:T(8,128)(2,1)S(1)} %get-tuple-element.62), channel_id=1, source_target_pairs={{0,32},{16,48},{32,64},{48,80},{64,96},{80,112},{96,0},{112,16},{2... | collective-permute-start | bytes 688136 | tf_op jit(solution)/shard_map/ppermute | solution.py:44
  89.7 3.9 %collective-permute-start.23 = (bf16[64,1792]{1,0:T(8,128)(2,1)S(1)}, bf16[64,1792]{1,0:T(8,128)(2,1)S(1)}, u32[]{:S(2)}, u32[]{:S(2)}) collective-permute-start(bf16[64,1792]{1,0:T(8,128)(2,1)S(1)} %get-tuple-element.63), channel_id=1, source_target_pairs={{0,112},{16,0},{32,16},{48,32},{64,48},{80,64},{96,80},{112,96},{2... | collective-permute-start | bytes 688136 | tf_op jit(solution)/shard_map/ppermute | solution.py:44
  93.6 1.4 %collective-permute-done.18.refs_2_ = bf16[64,1792]{1,0:T(8,128)(2,1)S(1)} collective-permute-done((bf16[64,1792]{1,0:T(8,128)(2,1)S(1)}, bf16[64,1792]{1,0:T(8,128)(2,1)S(1)}, u32[]{:S(2)}, u32[]{:S(2)}) %collective-permute-start.18) | collective-permute-done | bytes 229408 | tf_op jit(solution)/shard_map/ppermute | solution.py:44
  97.1 3.3 %collective-permute-done.21.refs_4_ = bf16[64,1792]{1,0:T(8,128)(2,1)S(1)} collective-permute-done((bf16[64,1792]{1,0:T(8,128)(2,1)S(1)}, bf16[64,1792]{1,0:T(8,128)(2,1)S(1)}, u32[]{:S(2)}, u32[]{:S(2)}) %collective-permute-start.21) | collective-permute-done | bytes 229408 | tf_op jit(solution)/shard_map/ppermute | solution.py:44
  102.0 2.2 %collective-permute-done.24.refs_4_ = bf16[64,1792]{1,0:T(8,128)(2,1)S(1)} collective-permute-done((bf16[64,1792]{1,0:T(8,128)(2,1)S(1)}, bf16[64,1792]{1,0:T(8,128)(2,1)S(1)}, u32[]{:S(2)}, u32[]{:S(2)}) %collective-permute-start.24) | collective-permute-done | bytes 229408 | tf_op jit(solution)/shard_map/ppermute | solution.py:44
  104.2 1.2 shard_map.129
  105.3 4.7 %all-to-all-start.1 = ((bf16[8,16,1792]{2,1,0:T(8,128)(2,1)}), bf16[8,16,1792]{2,1,0:T(8,128)(2,1)S(1)}, u32[]{:S(2)}, u32[]{:S(2)}) async-start(bf16[8,16,1792]{2,1,0:T(8,128)(2,1)} %shard_map.129), calls=%async_computation.1 | async-start | bytes 917504 | tf_op jit(solution)/shard_map/all_to_all | solution.py:469
  110.1 3.2 %shard_map.131 = bf16[4,32,512]{2,1,0:T(8,128)(2,1)} custom-call(s32[4]{0:T(128)S(1)} %copy-done.4, bf16[4,32,512]{2,1,0:T(8,128)(2,1)S(1)} %copy-done.1, bf16[4,32,64]{2,1,0:T(8,128)(2,1)S(1)} %copy-done.3, bf16[4,256,512]{2,1,0:T(8,128)(2,1)S(1)} %copy-done, bf16[4,64,256]{2,1,0:T(8,128)(2,1)S(1)} %copy-done.2), custom_call_target="tpu_custom_call" | custom-call | tf_op jit(solution)/shard_map/pallas_call | solution.py:52
  113.3 8.0 %all-to-all-done.1.share_ref = bf16[8,16,1792]{2,1,0:T(8,128)(2,1)S(1)} async-done(((bf16[8,16,1792]{2,1,0:T(8,128)(2,1)}), bf16[8,16,1792]{2,1,0:T(8,128)(2,1)S(1)}, u32[]{:S(2)}, u32[]{:S(2)}) %all-to-all-start.1) | async-done | bytes 458784 | tf_op jit(solution)/shard_map/all_to_all | solution.py:469
  (53 shorter events, 13.7 us)
Async XLA Ops:
  39.0 16.7 %collective-permute-start.1 = (bf16[64,1792]{1,0:T(8,128)(2,1)S(1)}, bf16[64,1792]{1,0:T(8,128)(2,1)S(1)}, u32[]{:S(2)}, u32[]{:S(2)}) collective-permute-start(bf16[64,1792]{1,0:T(8,128)(2,1)S(1)} %get-tuple-element.42), channel_id=1, source_target_pairs={{0,64},{16,80},{32,96},{48,112},{64,0},{80,16},{96,32},{112,48},{2... | collective-permute-start | bytes 688136 | tf_op jit(solution)/shard_map/ppermute | solution.py:44
  39.1 16.5 %collective-permute-start.2 = (bf16[64,1792]{1,0:T(8,128)(2,1)S(1)}, bf16[64,1792]{1,0:T(8,128)(2,1)S(1)}, u32[]{:S(2)}, u32[]{:S(2)}) collective-permute-start(bf16[64,1792]{1,0:T(8,128)(2,1)S(1)} %get-tuple-element.50), channel_id=1, source_target_pairs={{0,48},{16,64},{32,80},{48,96},{64,112},{80,0},{96,16},{112,32},{2... | collective-permute-start | bytes 688136 | tf_op jit(solution)/shard_map/ppermute | solution.py:44
  39.6 19.3 %collective-permute-start.3 = (bf16[64,1792]{1,0:T(8,128)(2,1)S(1)}, bf16[64,1792]{1,0:T(8,128)(2,1)S(1)}, u32[]{:S(2)}, u32[]{:S(2)}) collective-permute-start(bf16[64,1792]{1,0:T(8,128)(2,1)S(1)} %get-tuple-element.51), channel_id=1, source_target_pairs={{0,80},{16,96},{32,112},{48,0},{64,16},{80,32},{96,48},{112,64},{2... | collective-permute-start | bytes 688136 | tf_op jit(solution)/shard_map/ppermute | solution.py:44
  44.3 14.8 %collective-permute-start.4 = (bf16[64,1792]{1,0:T(8,128)(2,1)S(1)}, bf16[64,1792]{1,0:T(8,128)(2,1)S(1)}, u32[]{:S(2)}, u32[]{:S(2)}) collective-permute-start(bf16[64,1792]{1,0:T(8,128)(2,1)S(1)} %get-tuple-element.52), channel_id=1, source_target_pairs={{0,32},{16,48},{32,64},{48,80},{64,96},{80,112},{96,0},{112,16},{2... | collective-permute-start | bytes 688136 | tf_op jit(solution)/shard_map/ppermute | solution.py:44
  44.3 15.1 %collective-permute-start.5 = (bf16[64,1792]{1,0:T(8,128)(2,1)S(1)}, bf16[64,1792]{1,0:T(8,128)(2,1)S(1)}, u32[]{:S(2)}, u32[]{:S(2)}) collective-permute-start(bf16[64,1792]{1,0:T(8,128)(2,1)S(1)} %get-tuple-element.53), channel_id=1, source_target_pairs={{0,96},{16,112},{32,0},{48,16},{64,32},{80,48},{96,64},{112,80},{2... | collective-permute-start | bytes 688136 | tf_op jit(solution)/shard_map/ppermute | solution.py:44
  55.6 7.2 %collective-permute-start.6 = (bf16[64,1792]{1,0:T(8,128)(2,1)S(1)}, bf16[64,1792]{1,0:T(8,128)(2,1)S(1)}, u32[]{:S(2)}, u32[]{:S(2)}) collective-permute-start(bf16[64,1792]{1,0:T(8,128)(2,1)S(1)} %get-tuple-element.54), channel_id=1, source_target_pairs={{0,16},{16,32},{32,48},{48,64},{64,80},{80,96},{96,112},{112,0},{2... | collective-permute-start | bytes 688136 | tf_op jit(solution)/shard_map/ppermute | solution.py:44
  55.6 7.2 %collective-permute-start.7 = (bf16[64,1792]{1,0:T(8,128)(2,1)S(1)}, bf16[64,1792]{1,0:T(8,128)(2,1)S(1)}, u32[]{:S(2)}, u32[]{:S(2)}) collective-permute-start(bf16[64,1792]{1,0:T(8,128)(2,1)S(1)} %get-tuple-element.55), channel_id=1, source_target_pairs={{0,112},{16,0},{32,16},{48,32},{64,48},{80,64},{96,80},{112,96},{2... | collective-permute-start | bytes 688136 | tf_op jit(solution)/shard_map/ppermute | solution.py:44
  58.9 4.5 %collective-permute-start.15 = (bf16[64,1792]{1,0:T(8,128)(2,1)S(1)}, bf16[64,1792]{1,0:T(8,128)(2,1)S(1)}, u32[]{:S(2)}, u32[]{:S(2)}) collective-permute-start(bf16[64,1792]{1,0:T(8,128)(2,1)S(1)} %get-tuple-element.40.refs_5_.refs_11_), channel_id=1, source_target_pairs={{0,1},{1,0},{2,3},{3,2},{4,5},{5,4},{6,7},{7,6},{8,9},{9,8},{10,11... | collective-permute-start | bytes 688136 | tf_op jit(solution)/shard_map/ppermute | solution.py:48
  59.0 4.5 %collective-permute-start.8 = (bf16[64,1792]{1,0:T(8,128)(2,1)S(1)}, bf16[64,1792]{1,0:T(8,128)(2,1)S(1)}, u32[]{:S(2)}, u32[]{:S(2)}) collective-permute-start(bf16[64,1792]{1,0:T(8,128)(2,1)S(1)} %collective-permute-done.1.refs_4_), channel_id=1, source_target_pairs={{0,1},{1,0},{2,3},{3,2},{4,5},{5,4},{6,7},{7,6},{8,9},{9,8},{10,11... | collective-permute-start | bytes 688136 | tf_op jit(solution)/shard_map/ppermute | solution.py:48
  59.4 4.5 %collective-permute-start.9 = (bf16[64,1792]{1,0:T(8,128)(2,1)S(1)}, bf16[64,1792]{1,0:T(8,128)(2,1)S(1)}, u32[]{:S(2)}, u32[]{:S(2)}) collective-permute-start(bf16[64,1792]{1,0:T(8,128)(2,1)S(1)} %collective-permute-done.2.refs_5_), channel_id=1, source_target_pairs={{0,1},{1,0},{2,3},{3,2},{4,5},{5,4},{6,7},{7,6},{8,9},{9,8},{10,11... | collective-permute-start | bytes 688136 | tf_op jit(solution)/shard_map/ppermute | solution.py:48
  62.9 1.8 %collective-permute-start.11 = (bf16[64,1792]{1,0:T(8,128)(2,1)S(1)}, bf16[64,1792]{1,0:T(8,128)(2,1)S(1)}, u32[]{:S(2)}, u32[]{:S(2)}) collective-permute-start(bf16[64,1792]{1,0:T(8,128)(2,1)S(1)} %collective-permute-done.4.refs_7_), channel_id=1, source_target_pairs={{0,1},{1,0},{2,3},{3,2},{4,5},{5,4},{6,7},{7,6},{8,9},{9,8},{10,11... | collective-permute-start | bytes 688136 | tf_op jit(solution)/shard_map/ppermute | solution.py:48
  63.4 1.6 %collective-permute-start.12 = (bf16[64,1792]{1,0:T(8,128)(2,1)S(1)}, bf16[64,1792]{1,0:T(8,128)(2,1)S(1)}, u32[]{:S(2)}, u32[]{:S(2)}) collective-permute-start(bf16[64,1792]{1,0:T(8,128)(2,1)S(1)} %collective-permute-done.5.refs_8_), channel_id=1, source_target_pairs={{0,1},{1,0},{2,3},{3,2},{4,5},{5,4},{6,7},{7,6},{8,9},{9,8},{10,11... | collective-permute-start | bytes 688136 | tf_op jit(solution)/shard_map/ppermute | solution.py:48
  63.5 1.8 %collective-permute-start.13 = (bf16[64,1792]{1,0:T(8,128)(2,1)S(1)}, bf16[64,1792]{1,0:T(8,128)(2,1)S(1)}, u32[]{:S(2)}, u32[]{:S(2)}) collective-permute-start(bf16[64,1792]{1,0:T(8,128)(2,1)S(1)} %collective-permute-done.6.refs_9_), channel_id=1, source_target_pairs={{0,1},{1,0},{2,3},{3,2},{4,5},{5,4},{6,7},{7,6},{8,9},{9,8},{10,11... | collective-permute-start | bytes 688136 | tf_op jit(solution)/shard_map/ppermute | solution.py:48
  63.9 1.8 %collective-permute-start.14 = (bf16[64,1792]{1,0:T(8,128)(2,1)S(1)}, bf16[64,1792]{1,0:T(8,128)(2,1)S(1)}, u32[]{:S(2)}, u32[]{:S(2)}) collective-permute-start(bf16[64,1792]{1,0:T(8,128)(2,1)S(1)} %collective-permute-done.7.refs_10_), channel_id=1, source_target_pairs={{0,1},{1,0},{2,3},{3,2},{4,5},{5,4},{6,7},{7,6},{8,9},{9,8},{10,11... | collective-permute-start | bytes 688136 | tf_op jit(solution)/shard_map/ppermute | solution.py:48
  72.0 13.0 %collective-permute-start.20 = (bf16[5,64,1792]{2,1,0:T(8,128)(2,1)S(1)}, bf16[5,64,1792]{2,1,0:T(8,128)(2,1)S(1)}, u32[]{:S(2)}, u32[]{:S(2)}) collective-permute-start(bf16[5,64,1792]{2,1,0:T(8,128)(2,1)S(1)} %shard_map.126), channel_id=1, source_target_pairs={{0,1},{1,0},{2,3},{3,2},{4,5},{5,4},{6,7},{7,6},{8,9},{9,8},{10,11... | collective-permute-start | bytes 3440648 | tf_op jit(solution)/shard_map/ppermute | solution.py:48
  72.3 3.6 %collective-permute-start.16 = (bf16[3,64,1792]{2,1,0:T(8,128)(2,1)S(1)}, bf16[3,64,1792]{2,1,0:T(8,128)(2,1)S(1)}, u32[]{:S(2)}, u32[]{:S(2)}) collective-permute-start(bf16[3,64,1792]{2,1,0:T(8,128)(2,1)S(1)} %get-tuple-element.57), channel_id=1, source_target_pairs={{0,1},{1,0},{2,3},{3,2},{4,5},{5,4},{6,7},{7,6},{8,9},{9,8},{10,11... | collective-permute-start | bytes 2064392 | tf_op jit(solution)/shard_map/ppermute | solution.py:48
  77.0 12.7 %collective-permute-start.17 = (bf16[64,1792]{1,0:T(8,128)(2,1)S(1)}, bf16[64,1792]{1,0:T(8,128)(2,1)S(1)}, u32[]{:S(2)}, u32[]{:S(2)}) collective-permute-start(bf16[64,1792]{1,0:T(8,128)(2,1)S(1)} %get-tuple-element.58), channel_id=1, source_target_pairs={{0,64},{16,80},{32,96},{48,112},{64,0},{80,16},{96,32},{112,48},{2... | collective-permute-start | bytes 688136 | tf_op jit(solution)/shard_map/ppermute | solution.py:44
  81.2 13.9 %collective-permute-start.18 = (bf16[64,1792]{1,0:T(8,128)(2,1)S(1)}, bf16[64,1792]{1,0:T(8,128)(2,1)S(1)}, u32[]{:S(2)}, u32[]{:S(2)}) collective-permute-start(bf16[64,1792]{1,0:T(8,128)(2,1)S(1)} %get-tuple-element.59), channel_id=1, source_target_pairs={{0,80},{16,96},{32,112},{48,0},{64,16},{80,32},{96,48},{112,64},{2... | collective-permute-start | bytes 688136 | tf_op jit(solution)/shard_map/ppermute | solution.py:44
  81.2 15.9 %collective-permute-start.19 = (bf16[64,1792]{1,0:T(8,128)(2,1)S(1)}, bf16[64,1792]{1,0:T(8,128)(2,1)S(1)}, u32[]{:S(2)}, u32[]{:S(2)}) collective-permute-start(bf16[64,1792]{1,0:T(8,128)(2,1)S(1)} %get-tuple-element.60), channel_id=1, source_target_pairs={{0,48},{16,64},{32,80},{48,96},{64,112},{80,0},{96,16},{112,32},{2... | collective-permute-start | bytes 688136 | tf_op jit(solution)/shard_map/ppermute | solution.py:44
  86.4 14.0 %collective-permute-start.21 = (bf16[64,1792]{1,0:T(8,128)(2,1)S(1)}, bf16[64,1792]{1,0:T(8,128)(2,1)S(1)}, u32[]{:S(2)}, u32[]{:S(2)}) collective-permute-start(bf16[64,1792]{1,0:T(8,128)(2,1)S(1)} %get-tuple-element.61), channel_id=1, source_target_pairs={{0,96},{16,112},{32,0},{48,16},{64,32},{80,48},{96,64},{112,80},{2... | collective-permute-start | bytes 688136 | tf_op jit(solution)/shard_map/ppermute | solution.py:44
  87.7 13.1 %collective-permute-start.22 = (bf16[64,1792]{1,0:T(8,128)(2,1)S(1)}, bf16[64,1792]{1,0:T(8,128)(2,1)S(1)}, u32[]{:S(2)}, u32[]{:S(2)}) collective-permute-start(bf16[64,1792]{1,0:T(8,128)(2,1)S(1)} %get-tuple-element.62), channel_id=1, source_target_pairs={{0,32},{16,48},{32,64},{48,80},{64,96},{80,112},{96,0},{112,16},{2... | collective-permute-start | bytes 688136 | tf_op jit(solution)/shard_map/ppermute | solution.py:44
  89.7 12.2 %collective-permute-start.23 = (bf16[64,1792]{1,0:T(8,128)(2,1)S(1)}, bf16[64,1792]{1,0:T(8,128)(2,1)S(1)}, u32[]{:S(2)}, u32[]{:S(2)}) collective-permute-start(bf16[64,1792]{1,0:T(8,128)(2,1)S(1)} %get-tuple-element.63), channel_id=1, source_target_pairs={{0,112},{16,0},{32,16},{48,32},{64,48},{80,64},{96,80},{112,96},{2... | collective-permute-start | bytes 688136 | tf_op jit(solution)/shard_map/ppermute | solution.py:44
  95.1 9.1 %collective-permute-start.24 = (bf16[64,1792]{1,0:T(8,128)(2,1)S(1)}, bf16[64,1792]{1,0:T(8,128)(2,1)S(1)}, u32[]{:S(2)}, u32[]{:S(2)}) collective-permute-start(bf16[64,1792]{1,0:T(8,128)(2,1)S(1)} %get-tuple-element.64), channel_id=1, source_target_pairs={{0,16},{16,32},{32,48},{48,64},{64,80},{80,96},{96,112},{112,0},{2... | collective-permute-start | bytes 688136 | tf_op jit(solution)/shard_map/ppermute | solution.py:44
  105.3 15.9 %all-to-all-start.1 = ((bf16[8,16,1792]{2,1,0:T(8,128)(2,1)}), bf16[8,16,1792]{2,1,0:T(8,128)(2,1)S(1)}, u32[]{:S(2)}, u32[]{:S(2)}) async-start(bf16[8,16,1792]{2,1,0:T(8,128)(2,1)} %shard_map.129), calls=%async_computation.1 | async-start | bytes 917504 | tf_op jit(solution)/shard_map/all_to_all | solution.py:469
  (7 other events, 121.3 us)
